TPU v7x, 32 devices: a whole 2x2x4 slice. The times are simulated.
32 devices in a mesh: dp: 2 (over x), ctx: 16 (over z, y, core).
Axes of the slice: x: 2, y: 2, z: 4, core: 2. Of those that a mesh axis runs over, the one named last changes fastest.
Arguments:
- queries: bfloat16 [2, 2048, 2048], P('dp', 'ctx'), may hold values from -6 to 6
- keys: bfloat16 [2, 2048, 2048], P('dp', 'ctx'), may hold values from -6 to 6
- values: bfloat16 [2, 2048, 2048], P('dp', 'ctx'), may hold values from -6 to 6
- upstream: bfloat16 [2, 2048, 2048], P('dp', 'ctx'), may hold values from -6 to 6
- filters: float32 [2048, 2048], P('ctx'), may hold values from -0.125 to 0.125
- out_weight: bfloat16 [2048, 2048], P('ctx'), may hold values from -0.125 to 0.125
Outputs:
- grad_queries: bfloat16 [2, 2048, 2048], P('dp', 'ctx')
- grad_keys: bfloat16 [2, 2048, 2048], P('dp', 'ctx')
- grad_values: bfloat16 [2, 2048, 2048], P('dp', 'ctx')
- grad_filters: float32 [2048, 2048], P('ctx')
- grad_weight: float32 [2048, 2048], P('ctx')
All inputs are finite; a program needn't handle non-finite values.
Results may differ from a plain program's by a relative error of at most 0.019.
Values may be sent and summed in bfloat16 or wider, within the bound.
No kernel may reach another device: no remote copies, remote signals or barrier semaphores. Data moves between devices by JAX's collectives and lax.ppermute only.
A program may use at most 128 MiB of HBM per device.

v0:
```python
import functools
import math

import jax
import jax.numpy as jnp
import numpy as np
from jax import lax
from jax.experimental import pallas as pl
from jax.experimental.pallas import tpu as pltpu
from jax.sharding import PartitionSpec as P


INNER = 256
ROWS = 16
VMEM_LIMIT = 20 << 20
f32 = jnp.float32
bf16 = jnp.bfloat16


def cmul_const(z, c):
    re, im = z
    if abs(c.imag) < 1e-12:
        return (re, im) if abs(c.real - 1) < 1e-12 else (re * c.real, im * c.real)
    if abs(c.real) < 1e-12:
        if abs(c.imag - 1) < 1e-12:
            return (-im, re)
        if abs(c.imag + 1) < 1e-12:
            return (im, -re)
    return (re * c.real - im * c.imag, re * c.imag + im * c.real)


def root(n, k):
    angle = 2.0 * math.pi * (k % n) / n
    return complex(math.cos(angle), math.sin(angle))


def complex_dft(zs, sign):
    n = len(zs)
    if n == 1:
        return zs
    even = complex_dft(zs[0::2], sign)
    odd = complex_dft(zs[1::2], sign)
    turned = [cmul_const(odd[k], root(n, sign * k)) for k in range(n // 2)]
    low = [(e[0] + t[0], e[1] + t[1]) for e, t in zip(even, turned)]
    high = [(e[0] - t[0], e[1] - t[1]) for e, t in zip(even, turned)]
    return low + high


def real_dft(xs):
    n = len(xs)
    if n == 2:
        if xs[1] is None:
            return [(xs[0], None), (xs[0], None)]
        return [(xs[0] + xs[1], None), (xs[0] - xs[1], None)]
    half, quarter = n // 2, n // 4
    total = [a if b is None else a + b for a, b in zip(xs[:half], xs[half:])]
    delta = [a if b is None else a - b for a, b in zip(xs[:half], xs[half:])]
    out = [None] * (half + 1)
    for j, value in enumerate(real_dft(total)):
        out[2 * j] = value
    zs = [
        cmul_const((delta[m], -delta[m + quarter]), root(n, -m)) for m in range(quarter)
    ]
    for j, value in enumerate(complex_dft(zs, -1)):
        k = 4 * j + 1
        if k <= half:
            out[k] = value
        else:
            out[n - k] = (value[0], -value[1])
    return out


def real_inverse(zs):
    n = 2 * (len(zs) - 1)
    if n == 2:
        return [zs[0][0] + zs[1][0], zs[0][0] - zs[1][0]]
    even, odd = real_inverse(zs[0::2]), odd_part(zs)
    return [e + o for e, o in zip(even, odd)] + [e - o for e, o in zip(even, odd)]


def odd_part(zs):
    n = 2 * (len(zs) - 1)
    quarter = n // 4
    picked = []
    for j in range(quarter):
        k = 4 * j + 1
        picked.append(zs[k] if k <= n // 2 else (zs[n - k][0], -zs[n - k][1]))
    turned = [
        cmul_const(z, root(n, m)) for m, z in enumerate(complex_dft(picked, 1))
    ]
    return [2.0 * z[0] for z in turned] + [-2.0 * z[1] for z in turned]


def real_inverse_half(zs):
    return [e + o for e, o in zip(real_inverse(zs[0::2]), odd_part(zs))]


def dft_table(seq_len):
    total = 2 * seq_len
    radix = total // INNER
    k1 = np.arange(radix // 2 + 1)[:, None, None]
    k2 = np.arange(INNER)[None, :, None]
    n2 = np.arange(INNER)[None, None, :]
    angle = 2.0 * np.pi * (n2 * (k1 + radix * k2) % total) / total
    return np.stack([np.cos(angle), np.sin(angle)], axis=1).astype(jnp.bfloat16)


def dot(a, b, dims=((1,), (0,))):
    return lax.dot_general(a, b, (dims, ((), ())), preferred_element_type=f32)


def spectrum(load, table_ref, out_ref, top_ref, bot_ref, saved=None):
    copies = []
    count = out_ref.shape[0]
    lanes = out_ref.shape[2] // 2

    def body(i, carry):
        start = pl.multiple_of(i * ROWS, ROWS)
        rows = pl.ds(start, ROWS)
        blocks = [load(n1, start) for n1 in range(count - 1)]
        for k, (re, im) in enumerate(real_dft(blocks + [None] * (count - 1))):
            re = re.astype(bf16)
            if im is None:
                top_ref[k, rows, :lanes] = re
                bot_ref[k, rows, lanes:] = -re
            else:
                im = im.astype(bf16)
                top_ref[k, rows, :lanes] = re
                top_ref[k, rows, lanes:] = im
                bot_ref[k, rows, :lanes] = im
                bot_ref[k, rows, lanes:] = -re
        return carry

    lax.fori_loop(0, INNER // ROWS, body, 0)
    for k in range(count):
        if k == 0 or k == count - 1:
            out_ref[k, :, :lanes] = dot(table_ref[k, 0], top_ref[k, :, :lanes])
            out_ref[k, :, lanes:] = dot(table_ref[k, 1], bot_ref[k, :, lanes:])
        else:
            out_ref[k] = dot(table_ref[k, 0], top_ref[k]) + dot(table_ref[k, 1], bot_ref[k])
        if saved is not None:
            copies.append(pltpu.make_async_copy(out_ref.at[k], saved[0].at[k], saved[1].at[k]))
            copies[-1].start()
    return copies


def product_inverse(a_ref, b_ref, conj_a, table_ref, z_ref, top_ref, bot_ref, store):
    count = a_ref.shape[0]
    lanes = a_ref.shape[2] // 2
    total = 2 * (count - 1) * INNER
    for k in range(count):
        ar, ai = a_ref[k, :, :lanes], a_ref[k, :, lanes:]
        br, bi = b_ref[k, :, :lanes], b_ref[k, :, lanes:]
        if conj_a:
            re, im = ar * br + ai * bi, ar * bi - ai * br
        else:
            re, im = ar * br - ai * bi, ar * bi + ai * br
        re, im = re.astype(bf16), im.astype(bf16)
        top_ref[k, :, :lanes] = re
        bot_ref[k, :, :lanes] = -im
        if 0 < k < count - 1:
            top_ref[k, :, lanes:] = im
            bot_ref[k, :, lanes:] = re
    turn = ((0,), (0,))
    for k in range(count):
        if k == 0 or k == count - 1:
            z_ref[k, :, :lanes] = dot(table_ref[k, 0], top_ref[k, :, :lanes], turn) + dot(
                table_ref[k, 1], bot_ref[k, :, :lanes], turn
            )
        else:
            z_ref[k] = dot(table_ref[k, 0], top_ref[k], turn) + dot(
                table_ref[k, 1], bot_ref[k], turn
            )

    def body(i, carry):
        start = pl.multiple_of(i * ROWS, ROWS)
        rows = pl.ds(start, ROWS)
        zs = []
        for k in range(count):
            re = z_ref[k, rows, :lanes]
            zs.append((re, None if k in (0, count - 1) else z_ref[k, rows, lanes:]))
        for n1, value in enumerate(real_inverse_half(zs)):
            store(n1, start, value * (1.0 / total))
        return carry

    lax.fori_loop(0, INNER // ROWS, body, 0)


def filter_kernel(filters_ref, table_ref, saved_ref, spec_ref, turned_ref, top_ref, bot_ref, sems):
    count = spec_ref.shape[0]
    for n1 in range(count - 1):
        turned_ref[n1] = filters_ref[:, n1 * INNER : (n1 + 1) * INNER].T
    for copy in spectrum(
        lambda n1, start: turned_ref[n1, pl.ds(start, ROWS)],
        table_ref,
        spec_ref,
        top_ref,
        bot_ref,
        (saved_ref, sems),
    ):
        copy.wait()


def conv_kernel(
    got_ref,
    filters_ref,
    table_ref,
    conv_ref,
    gated_ref,
    saved_ref,
    filt_ref,
    spec_ref,
    z_ref,
    top_ref,
    bot_ref,
    sems,
    sem,
):
    local_t = got_ref.shape[2]
    fetch = pltpu.make_async_copy(filters_ref, filt_ref, sem)
    fetch.start()

    def load(kind, token):
        here = pl.ds(pl.multiple_of(token % local_t, ROWS), ROWS)
        return got_ref[token // local_t, kind, here].astype(f32)

    copies = spectrum(
        lambda n1, start: load(0, n1 * INNER + start),
        table_ref,
        spec_ref,
        top_ref,
        bot_ref,
        (saved_ref, sems),
    )
    fetch.wait()

    def store(n1, start, value):
        rows = pl.ds(n1 * INNER + start, ROWS)
        value = value.astype(bf16)
        conv_ref[rows] = value
        query = load(1, n1 * INNER + start)
        gated_ref[rows] = (query * value.astype(f32)).astype(bf16)

    product_inverse(filt_ref, spec_ref, False, table_ref, z_ref, top_ref, bot_ref, store)
    for copy in copies:
        copy.wait()


def grad_kernel(n_chunks, *refs):
    chunk_refs, (weight_ref, out_ref, rows_ref) = refs[:n_chunks], refs[n_chunks:]
    rows = chunk_refs[0].shape[0]
    for i, ref in enumerate(chunk_refs):
        rows_ref[i * rows : (i + 1) * rows] = ref[...]
    out_ref[...] = dot(rows_ref[...], weight_ref[...], ((1,), (1,))).astype(bf16)


def split_kernel(key_ref, value_ref, query_ref, out_ref):
    n, _, _, chan = out_ref.shape
    for p in range(n):
        cols = slice(p * chan, (p + 1) * chan)
        mixed = key_ref[:, cols].astype(f32) * value_ref[:, cols].astype(f32)
        out_ref[p, 0] = mixed.astype(bf16)
        out_ref[p, 1] = query_ref[:, cols]


def finish_kernel(got_ref, key_ref, value_ref, grad_query_ref, grad_key_ref, grad_value_ref):
    n, _, _, chan = got_ref.shape
    for p in range(n):
        cols = slice(p * chan, (p + 1) * chan)
        grad_query_ref[:, cols] = got_ref[p, 0]
        back = got_ref[p, 1].astype(f32)
        grad_key_ref[:, cols] = (back * value_ref[:, cols].astype(f32)).astype(bf16)
        grad_value_ref[:, cols] = (back * key_ref[:, cols].astype(f32)).astype(bf16)


def tail_kernel(n_parts, n_chunks, where_ref, *refs):
    part_refs, refs = refs[:n_parts], refs[n_parts:]
    chunk_refs, refs = refs[:n_chunks], refs[n_chunks:]
    weight_ref, got_ref, conv_ref, filters_ref, table_ref, *refs = refs
    out_ref, saved_ref, scaled_ref, rows_ref, grad_ref, *refs = refs
    filt_ref, spec_ref, z_ref, top_ref, bot_ref, sems, sem = refs
    fetch = pltpu.make_async_copy(filters_ref, filt_ref, sem)
    fetch.start()
    rows = chunk_refs[0].shape[0]
    _, _, local_t, _ = out_ref.shape
    halves = local_t // rows
    weight = weight_ref[...]
    i = 0

    def scale(grad, unit):
        block, start = unit // halves, pl.multiple_of(unit % halves * rows, rows)
        here, place = pl.ds(start, rows), pl.ds(pl.multiple_of(unit * rows, rows), rows)
        query = got_ref[block, 1, here].astype(f32)
        scaled_ref[place] = (grad * query).astype(bf16)
        out_ref[block, 0, here] = (grad * conv_ref[place].astype(f32)).astype(bf16)

    for ref in part_refs:
        for j in range(ref.shape[0] // rows):
            scale(ref[j * rows : (j + 1) * rows].astype(f32), where_ref[i])
            i += 1
    for j, ref in enumerate(chunk_refs):
        rows_ref[j * rows : (j + 1) * rows] = ref[...]
    grad_ref[...] = dot(rows_ref[...], weight, ((1,), (1,))).astype(bf16)
    for j in range(n_chunks):
        scale(grad_ref[j * rows : (j + 1) * rows].astype(f32), where_ref[i + j])
    copies = spectrum(
        lambda n1, start: scaled_ref[pl.ds(n1 * INNER + start, ROWS)].astype(f32),
        table_ref,
        spec_ref,
        top_ref,
        bot_ref,
        (saved_ref, sems),
    )
    fetch.wait()

    def store(n1, start, value):
        token = n1 * INNER + start
        here = pl.ds(pl.multiple_of(token % local_t, ROWS), ROWS)
        out_ref[token // local_t, 1, here] = value.astype(bf16)

    product_inverse(filt_ref, spec_ref, True, table_ref, z_ref, top_ref, bot_ref, store)
    for copy in copies:
        copy.wait()


def taps_kernel(
    saved_mix, saved_grad, table_ref, out_ref, mix_ref, grad_ref, z_ref, top_ref, bot_ref, turned_ref, sems
):
    fetch = [
        pltpu.make_async_copy(saved_mix, mix_ref, sems.at[0]),
        pltpu.make_async_copy(saved_grad, grad_ref, sems.at[1]),
    ]
    for copy in fetch:
        copy.start()
    for copy in fetch:
        copy.wait()

    def store(n1, start, value):
        turned_ref[n1, pl.ds(start, ROWS)] = value

    product_inverse(mix_ref, grad_ref, True, table_ref, z_ref, top_ref, bot_ref, store)
    for n1 in range(mix_ref.shape[0] - 1):
        out_ref[:, n1 * INNER : (n1 + 1) * INNER] = turned_ref[n1].T.astype(bf16)


def weight_kernel(n_chunks, first, unit, where_ref, *refs):
    chunk_refs, rest = refs[:n_chunks], refs[n_chunks:]
    gated_ref, rest = rest[0], rest[1:]
    if not first:
        sum_ref, rest = rest[0], rest[1:]
    (out_ref,) = rest
    gated, i = [], 0
    for ref in chunk_refs:
        for _ in range(ref.shape[0] // unit):
            gated.append(gated_ref[pl.ds(pl.multiple_of(where_ref[i] * unit, unit), unit)])
            i += 1
    left = jnp.concatenate(gated, axis=0)
    width = chunk_refs[0].shape[1]
    step = 512 if width % 512 == 0 else width
    for c in range(0, width, step):
        right = jnp.concatenate([r[:, c : c + step] for r in chunk_refs], axis=0)
        acc = dot(left, right, ((0,), (0,)))
        if not first:
            acc = acc + sum_ref[:, c : c + step]
        out_ref[:, c : c + step] = acc.astype(out_ref.dtype)


def vmem():
    return pl.BlockSpec(memory_space=pltpu.VMEM)


def hbm():
    return pl.BlockSpec(memory_space=pltpu.HBM)


def smem():
    return pl.BlockSpec(memory_space=pltpu.SMEM)


def in_hbm(x):
    return pltpu.with_memory_space_constraint(x, pltpu.HBM)


def call(kernel, outs, n_in, scratch=(), scalars=0, flops=0, kept=(), saved=None):
    ins = [hbm() if i in kept else vmem() for i in range(n_in)]
    many = isinstance(outs, tuple)
    specs = [hbm() if i == saved else vmem() for i in range(len(outs) if many else 1)]
    return pl.pallas_call(
        kernel,
        out_shape=outs,
        in_specs=[smem()] * scalars + ins,
        out_specs=tuple(specs) if many else specs[0],
        scratch_shapes=list(scratch),
        compiler_params=pltpu.CompilerParams(vmem_limit_bytes=VMEM_LIMIT),
        cost_estimate=pl.CostEstimate(flops=flops, bytes_accessed=1 << 20, transcendentals=0),
    )


def chip_cycle(chips):
    rows = 1 << (chips.bit_length() // 2)
    while chips % rows:
        rows //= 2
    cols = chips // rows
    if cols == 1 or rows % 2:
        return list(range(chips))
    order = [r * cols for r in range(rows)]
    for i, r in enumerate(reversed(range(rows))):
        across = list(range(1, cols))
        order += [r * cols + c for c in (across if i % 2 == 0 else reversed(across))]
    return order


def per_device(size, queries, keys, values, upstream, filters, out_weight):
    chips = size // 2
    cycle = chip_cycle(chips)
    place = {chip: i for i, chip in enumerate(cycle)}
    forward = []
    for i, chip in enumerate(cycle):
        for core in range(2):
            forward.append((2 * chip + core, 2 * cycle[(i + 1) % chips] + core))
    backward = [(b, a) for a, b in forward]
    partner = [(i, i ^ 1) for i in range(size)]

    def sources(offset, other):
        table = []
        for p in range(size):
            chip = cycle[(place[p // 2] + offset) % chips]
            table.append(2 * chip + ((p % 2) ^ other))
        return table

    rows, queries_rows = upstream[0], queries[0]
    key_rows, value_rows = keys[0], values[0]
    local_t, width = rows.shape
    chan = out_weight.shape[0]
    seq_len = filters.shape[1]
    count = seq_len // INNER + 1
    table = jnp.asarray(dft_table(seq_len))
    spec = pltpu.HBM((count, INNER, 2 * chan), f32)
    chan_bf = pltpu.HBM((seq_len, chan), bf16)
    sem, sems = pltpu.SemaphoreType.DMA(()), pltpu.SemaphoreType.DMA((count,))
    top = pltpu.VMEM((count, INNER, 2 * chan), bf16)
    zs = pltpu.VMEM((count, INNER, 2 * chan), f32)
    turned = pltpu.VMEM((count - 1, INNER, chan), f32)
    one = 8 * count * INNER * INNER * chan

    half = local_t // 2
    steps = chips // 2
    me = lax.axis_index("ctx")

    def to_partner(x):
        return lax.ppermute(x, "ctx", partner)

    def exchange(x):
        return lax.all_to_all(x, "ctx", 0, 0, tiled=True)

    def grad_of(group):
        n = len(group)
        return call(
            functools.partial(grad_kernel, n),
            pltpu.HBM((n * local_t, chan), bf16),
            n + 1,
            [pltpu.VMEM((n * local_t, width), bf16)],
            flops=2 * n * local_t * width * chan,
        )(*[g[0] for g in group], out_weight)

    def pair(x, offset, halves=(0, 1)):
        return [(x, offset, 0, halves), (to_partner(x), offset, 1, halves)]

    blocks = pltpu.HBM((size, 2, local_t, chan), bf16)
    send = call(split_kernel, blocks, 3, flops=seq_len * chan)(
        in_hbm(key_rows), in_hbm(value_rows), in_hbm(queries_rows)
    )
    got = exchange(send)
    filt_spec = call(filter_kernel, spec, 2, [zs, turned, top, top, sems], flops=one, saved=0)(
        in_hbm(filters), table
    )
    groups = [pair(rows, 0)]
    parts = []
    ahead, behind = rows, rows
    for step in range(1, steps):
        ahead = lax.ppermute(ahead, "ctx", forward)
        behind = lax.ppermute(behind, "ctx", backward)
        groups.append(pair(ahead, -step) + pair(behind, step))
        parts.append(grad_of(groups[step - 1]))
    ahead = lax.ppermute(ahead[:half], "ctx", forward)
    behind = lax.ppermute(behind[half:], "ctx", backward)
    parts.append(grad_of(groups[-1]))
    conv_chan, gated_chan, mix_spec = call(
        conv_kernel,
        (chan_bf, chan_bf, spec),
        3,
        [zs, zs, zs, top, top, sems, sem],
        flops=2 * one,
        kept=(1,),
        saved=2,
    )(got, in_hbm(filt_spec), table)
    groups.append(pair(ahead, -steps, (0,)) + pair(behind, -steps, (1,)))

    where = [[2 * p + h for p in sources(g[1], g[2])] for group in groups for g in group for h in g[3]]
    where = jnp.asarray(np.array(where, np.int32).T)[me]

    first = [g[0] for group in groups[:-1] for g in group]
    final = [g[0] for g in groups[-1]]
    total = call(
        functools.partial(weight_kernel, len(first), True, half),
        pltpu.VMEM((chan, width), f32),
        len(first) + 1,
        scalars=1,
        flops=2 * len(first) * local_t * width * chan,
    )(where[: -len(final)], *first, gated_chan)

    back, grad_spec = call(
        functools.partial(tail_kernel, len(parts), len(final)),
        (blocks, spec),
        len(parts) + len(final) + 5,
        [
            pltpu.VMEM((seq_len, chan), bf16),
            pltpu.VMEM((len(final) * half, width), bf16),
            pltpu.VMEM((len(final) * half, chan), bf16),
            zs,
            zs,
            zs,
            top,
            top,
            sems,
            sem,
        ],
        scalars=1,
        flops=2 * one,
        kept=(len(parts) + len(final) + 3,),
        saved=1,
    )(where, *parts, *final, out_weight, got, conv_chan, in_hbm(filt_spec), table)
    back = exchange(back)

    part_weight = call(
        functools.partial(weight_kernel, len(final), False, half),
        jax.ShapeDtypeStruct((chan, width), bf16),
        len(final) + 2,
        scalars=1,
        flops=2 * len(final) * half * width * chan,
    )(where[-len(final) :], *final, gated_chan, total)
    taps = call(
        taps_kernel,
        jax.ShapeDtypeStruct((chan, seq_len), bf16),
        3,
        [zs, zs, zs, top, top, turned, pltpu.SemaphoreType.DMA((2,))],
        flops=one,
        kept=(0, 1),
    )(in_hbm(mix_spec), in_hbm(grad_spec), table)
    rows_bf = jax.ShapeDtypeStruct((local_t, size * chan), bf16)
    grad_queries, grad_keys, grad_values = call(
        finish_kernel, (rows_bf, rows_bf, rows_bf), 3, flops=seq_len * chan
    )(back, key_rows, value_rows)

    def over_dp(x):
        n = lax.axis_size("dp")
        total = x.astype(f32)
        if n == 2:
            return total + lax.ppermute(x, "dp", [(0, 1), (1, 0)]).astype(f32)
        return lax.psum(x, "dp").astype(f32)

    return (
        grad_queries[None], grad_keys[None], grad_values[None], over_dp(taps), over_dp(part_weight)
    )


def solution(mesh):
    tokens, chans = P("dp", "ctx", None), P("ctx", None)

    def body(*args):
        return per_device(mesh.shape["ctx"], *args)

    return jax.shard_map(
        body,
        mesh=mesh,
        in_specs=(tokens, tokens, tokens, tokens, chans, chans),
        out_specs=(tokens, tokens, tokens, chans, chans),
        check_vma=False,
    )
```

profile of v0, /device:TPU:0, one launch (start us, length us, event | category | flops | bytes accessed | tf_op | source)
XLA Modules:
  0.0 154.5 jit_solution(8582261350228667361)
XLA Ops:
  0.6 3.0 %collective-permute-start.3 = (bf16[128,2048]{1,0:T(8,128)(2,1)}, bf16[128,2048]{1,0:T(8,128)(2,1)S(1)}, u32[]{:S(2)}, u32[]{:S(2)}) collective-permute-start(bf16[128,2048]{1,0:T(8,128)(2,1)} %bitcast.13), channel_id=1, source_target_pairs={{4,0},{5,1},{8,4},{9,5},{12,8},{13,9},{14,12},{15,13},{10,14},{11,... | collective-permute-start | bytes 1572872 | tf_op jit(solution)/shard_map/ppermute | solution.py:482
  3.8 12.1 %collective-permute-done.3.refs_2_.refs_4_ = bf16[128,2048]{1,0:T(8,128)(2,1)S(1)} collective-permute-done((bf16[128,2048]{1,0:T(8,128)(2,1)}, bf16[128,2048]{1,0:T(8,128)(2,1)S(1)}, u32[]{:S(2)}, u32[]{:S(2)}) %collective-permute-start.3) | collective-permute-done | bytes 524320 | tf_op jit(solution)/shard_map/ppermute | solution.py:482
  15.9 1.7 %collective-permute-start.7 = (bf16[128,2048]{1,0:T(8,128)(2,1)S(1)}, bf16[128,2048]{1,0:T(8,128)(2,1)}, u32[]{:S(2)}, u32[]{:S(2)}) collective-permute-start(bf16[128,2048]{1,0:T(8,128)(2,1)S(1)} %collective-permute-done.3.refs_2_.refs_4_), channel_id=1, source_target_pairs={{4,0},{5,1},{8,4},{9,5},{12,8},{13,9},{14,12},{15,13},{10,14},{11,... | collective-permute-start | bytes 1572872 | tf_op jit(solution)/shard_map/ppermute | solution.py:482
  17.6 2.7 %shard_map.123 = bf16[16,2,128,128]{3,2,1,0:T(8,128)(2,1)} custom-call(bf16[128,2048]{1,0:T(8,128)(2,1)} %bitcast.18, bf16[128,2048]{1,0:T(8,128)(2,1)} %bitcast.20, bf16[128,2048]{1,0:T(8,128)(2,1)} %bitcast.22), custom_call_target="tpu_custom_call" | custom-call | flops 262144 | bytes 1048576 | tf_op jit(solution)/shard_map/pallas_call | solution.py:470
  20.2 5.0 %all-to-all-start = ((bf16[16,2,128,128]{3,2,1,0:T(8,128)(2,1)}), bf16[16,2,128,128]{3,2,1,0:T(8,128)(2,1)}, u32[]{:S(2)}, u32[]{:S(2)}) async-start(bf16[16,2,128,128]{3,2,1,0:T(8,128)(2,1)} %shard_map.123), calls=%async_computation | async-start | bytes 2097152 | tf_op jit(solution)/shard_map/all_to_all | solution.py:454
  25.3 1.9 %collective-permute-start.5 = (bf16[128,2048]{1,0:T(8,128)(2,1)}, bf16[128,2048]{1,0:T(8,128)(2,1)}, u32[]{:S(2)}, u32[]{:S(2)}) collective-permute-start(bf16[128,2048]{1,0:T(8,128)(2,1)} %collective-permute-done.1.refs_0_.refs_2_), channel_id=1, source_target_pairs={{0,4},{1,5},{4,8},{5,9},{8,12},{9,13},{12,14},{13,15},{14,10},{15,... | collective-permute-start | bytes 1572872 | tf_op jit(solution)/shard_map/ppermute | solution.py:481
  27.2 3.6 %collective-permute-done.7.refs_2_.refs_8_ = bf16[128,2048]{1,0:T(8,128)(2,1)} collective-permute-done((bf16[128,2048]{1,0:T(8,128)(2,1)S(1)}, bf16[128,2048]{1,0:T(8,128)(2,1)}, u32[]{:S(2)}, u32[]{:S(2)}) %collective-permute-start.7) | collective-permute-done | bytes 524320 | tf_op jit(solution)/shard_map/ppermute | solution.py:482
  30.8 1.5 collective-permute-start.11
  32.3 22.4 %collective-permute-done.5.refs_0_.refs_6_ = bf16[128,2048]{1,0:T(8,128)(2,1)} collective-permute-done((bf16[128,2048]{1,0:T(8,128)(2,1)}, bf16[128,2048]{1,0:T(8,128)(2,1)}, u32[]{:S(2)}, u32[]{:S(2)}) %collective-permute-start.5) | collective-permute-done | bytes 524320 | tf_op jit(solution)/shard_map/ppermute | solution.py:481
  54.7 7.2 %collective-permute-start.9 = (bf16[128,2048]{1,0:T(8,128)(2,1)}, bf16[128,2048]{1,0:T(8,128)(2,1)}, u32[]{:S(2)}, u32[]{:S(2)}) collective-permute-start(bf16[128,2048]{1,0:T(8,128)(2,1)} %collective-permute-done.5.refs_0_.refs_6_), channel_id=1, source_target_pairs={{0,4},{1,5},{4,8},{5,9},{8,12},{9,13},{12,14},{13,15},{14,10},{15,... | collective-permute-start | bytes 1572872 | tf_op jit(solution)/shard_map/ppermute | solution.py:481
  62.8 10.2 %collective-permute-done.9.refs_0_.refs_10_ = bf16[128,2048]{1,0:T(8,128)(2,1)} collective-permute-done((bf16[128,2048]{1,0:T(8,128)(2,1)}, bf16[128,2048]{1,0:T(8,128)(2,1)}, u32[]{:S(2)}, u32[]{:S(2)}) %collective-permute-start.9) | collective-permute-done | bytes 524320 | tf_op jit(solution)/shard_map/ppermute | solution.py:481
  73.7 1.7 %slice.24 = bf16[64,2048]{1,0:T(8,128)(2,1)} slice(bf16[128,2048]{1,0:T(8,128)(2,1)} %collective-permute-done.9.refs_0_.refs_10_), slice={[0:64], [0:2048]} | slice | bytes 524288 | tf_op jit(solution)/shard_map/slice | solution.py:485
  76.2 4.0 %collective-permute-start.15 = (bf16[64,2048]{1,0:T(8,128)(2,1)}, bf16[64,2048]{1,0:T(8,128)(2,1)}, u32[]{:S(2)}, u32[]{:S(2)}) collective-permute-start(bf16[64,2048]{1,0:T(8,128)(2,1)} %slice.25), channel_id=1, source_target_pairs={{4,0},{5,1},{8,4},{9,5},{12,8},{13,9},{14,12},{15,13},{10,14},{11,... | collective-permute-start | bytes 786440 | tf_op jit(solution)/shard_map/ppermute | solution.py:486
  83.1 3.7 %collective-permute-done.15.refs_6_.refs_2_ = bf16[64,2048]{1,0:T(8,128)(2,1)} collective-permute-done((bf16[64,2048]{1,0:T(8,128)(2,1)}, bf16[64,2048]{1,0:T(8,128)(2,1)}, u32[]{:S(2)}, u32[]{:S(2)}) %collective-permute-start.15) | collective-permute-done | bytes 262176 | tf_op jit(solution)/shard_map/ppermute | solution.py:486
  86.8 3.0 %collective-permute-done.13.refs_4_.refs_0_ = bf16[64,2048]{1,0:T(8,128)(2,1)} collective-permute-done((bf16[64,2048]{1,0:T(8,128)(2,1)}, bf16[64,2048]{1,0:T(8,128)(2,1)}, u32[]{:S(2)}, u32[]{:S(2)}) %collective-permute-start.13) | collective-permute-done | bytes 262176 | tf_op jit(solution)/shard_map/ppermute | solution.py:485
  90.6 4.1 %shard_map.124.filters_ref.refs_11_ = f32[9,256,256]{2,1,0:T(8,128)} custom-call(f32[128,2048]{1,0:T(8,128)} %filters_ref.1, bf16[9,2,256,256]{3,2,1,0:T(8,128)(2,1)S(1)} %copy-done), custom_call_target="tpu_custom_call" | custom-call | flops 603979776 | bytes 1048576 | tf_op jit(solution)/shard_map/pallas_call | solution.py:474
  94.7 1.1 shard_map.119.refs_0_
  95.7 2.4 %shard_map.120.refs_1_ = bf16[512,128]{1,0:T(8,128)(2,1)} custom-call(bf16[128,2048]{1,0:T(8,128)(2,1)} %collective-permute-done.1.refs_0_.refs_2_, bf16[128,2048]{1,0:T(8,128)(2,1)S(1)} %copy-done.19, bf16[128,2048]{1,0:T(8,128)(2,1)S(1)} %copy-done.13, bf16[128,2048]{1,0:T(8,128)(2,1)S(1)} %copy-done.16, bf16[128,2048]{1,0:T(8,128)(2,1)S(1)} %copy-done.1), custom_call_target="tpu_custom_call" | custom-call | flops 268435456 | bytes 1048576 | tf_op jit(solution)/shard_map/pallas_call | solution.py:458
  98.1 2.7 %shard_map.121.refs_2_ = bf16[512,128]{1,0:T(8,128)(2,1)} custom-call(bf16[128,2048]{1,0:T(8,128)(2,1)} %collective-permute-done.5.refs_0_.refs_6_, bf16[128,2048]{1,0:T(8,128)(2,1)} %collective-permute-done.6.refs_1_.refs_7_, bf16[128,2048]{1,0:T(8,128)(2,1)} %collective-permute-done.7.refs_2_.refs_8_, bf16[128,2048]{1,0:T(8,128)(2,1)S(1)} %copy-done.22, ...), custom_call_target="tpu_custom_call" | custom-call | flops 268435456 | bytes 1048576 | tf_op jit(solution)/shard_map/pallas_call | solution.py:458
  100.9 6.4 %shard_map.125 = (bf16[2048,128]{1,0:T(8,128)(2,1)}, bf16[2048,128]{1,0:T(8,128)(2,1)}, f32[9,256,256]{2,1,0:T(8,128)}) custom-call(bf16[16,2,128,128]{3,2,1,0:T(8,128)(2,1)} %all-to-all-done.got_ref.refs_9_, f32[9,256,256]{2,1,0:T(8,128)} %shard_map.124.filters_ref.refs_11_, bf16[9,2,256,256]{3,2,1,0:T(8,128)(2,1)S(1)} %copy-done), custom_call_target="tpu_custom_call" | custom-call | flops 1207959552 | bytes 1048576 | tf_op jit(solution)/shard_map/pallas_call | solution.py:488
  107.4 2.8 %shard_map.122.refs_3_ = bf16[512,128]{1,0:T(8,128)(2,1)} custom-call(bf16[128,2048]{1,0:T(8,128)(2,1)} %collective-permute-done.9.refs_0_.refs_10_, bf16[128,2048]{1,0:T(8,128)(2,1)} %collective-permute-done.10.refs_1_.refs_11_, bf16[128,2048]{1,0:T(8,128)(2,1)S(1)} %collective-permute-done.11.refs_2_.refs_12_, ...), custom_call_target="tpu_custom_call" | custom-call | flops 268435456 | bytes 1048576 | tf_op jit(solution)/shard_map/pallas_call | solution.py:458
  111.2 7.1 %shard_map.126 = (bf16[16,2,128,128]{3,2,1,0:T(8,128)(2,1)}, f32[9,256,256]{2,1,0:T(8,128)}) custom-call(s32[32]{0:T(128)S(1)} %get-tuple-element.22.where_ref, bf16[256,128]{1,0:T(8,128)(2,1)S(1)} %copy-done.29, bf16[512,128]{1,0:T(8,128)(2,1)S(1)} %copy-done.25, bf16[512,128]{1,0:T(8,128)(2,1)S(1)} %copy-done.26, bf16[512,128]{1,0:T(8,128)(2,1)S(1)} %copy-done.27, ...), custom_call_target="tpu_custom_call" | custom-call | flops 1207959552 | bytes 1048576 | tf_op jit(solution)/shard_map/pallas_call | solution.py:512
  118.2 3.8 %all-to-all-start.1 = ((bf16[16,2,128,128]{3,2,1,0:T(8,128)(2,1)}), bf16[16,2,128,128]{3,2,1,0:T(8,128)(2,1)S(1)}, u32[]{:S(2)}, u32[]{:S(2)}) async-start(bf16[16,2,128,128]{3,2,1,0:T(8,128)(2,1)} %get-tuple-element.14), calls=%async_computation.1 | async-start | bytes 2097152 | tf_op jit(solution)/shard_map/all_to_all | solution.py:454
  122.2 4.3 %shard_map.128 = bf16[128,2048]{1,0:T(8,128)(2,1)S(1)} custom-call(f32[9,256,256]{2,1,0:T(8,128)} %get-tuple-element.18.saved_mix, f32[9,256,256]{2,1,0:T(8,128)} %get-tuple-element.19.saved_grad, bf16[9,2,256,256]{3,2,1,0:T(8,128)(2,1)S(1)} %copy-done), custom_call_target="tpu_custom_call" | custom-call | flops 603979776 | bytes 1048576 | tf_op jit(solution)/shard_map/pallas_call | solution.py:542
  126.4 1.6 %collective-permute-start.17 = (bf16[128,2048]{1,0:T(8,128)(2,1)S(1)}, bf16[128,2048]{1,0:T(8,128)(2,1)S(1)}, u32[]{:S(2)}, u32[]{:S(2)}) collective-permute-start(bf16[128,2048]{1,0:T(8,128)(2,1)S(1)} %shard_map.128), channel_id=1, source_target_pairs={{0,16},{16,0},{1,17},{17,1},{2,18},{18,2},{3,19},{19,3},{4,20},{20... | collective-permute-start | bytes 1572872 | tf_op jit(solution)/shard_map/ppermute | solution.py:559
  128.1 3.2 %shard_map.129.refs_5_ = f32[128,2048]{1,0:T(8,128)S(1)} custom-call(s32[28]{0:T(128)S(1)} %slice_bitcast_fusion.where_ref, bf16[128,2048]{1,0:T(8,128)(2,1)S(1)} %bitcast.17, bf16[128,2048]{1,0:T(8,128)(2,1)S(1)} %copy-done.9, bf16[128,2048]{1,0:T(8,128)(2,1)} %collective-permute-done.1.refs_0_.refs_2_, bf16[128,2048]{1,0:T(8,128)(2,1)S(1)} %copy-done.20, ...), custom_call_target="tpu_custom_call" | custom-call | flops 939524096 | bytes 1048576 | tf_op jit(solution)/shard_map/pallas_call | solution.py:504
  131.3 1.5 shard_map.130
  133.5 7.8 %collective-permute-done.17 = bf16[128,2048]{1,0:T(8,128)(2,1)S(1)} collective-permute-done((bf16[128,2048]{1,0:T(8,128)(2,1)S(1)}, bf16[128,2048]{1,0:T(8,128)(2,1)S(1)}, u32[]{:S(2)}, u32[]{:S(2)}) %collective-permute-start.17) | collective-permute-done | bytes 524320 | tf_op jit(solution)/shard_map/ppermute | solution.py:559
  141.3 1.1 convert_add_fusion.1
  142.4 9.6 %collective-permute-done.18 = bf16[128,2048]{1,0:T(8,128)(2,1)S(1)} collective-permute-done((bf16[128,2048]{1,0:T(8,128)(2,1)S(1)}, bf16[128,2048]{1,0:T(8,128)(2,1)S(1)}, u32[]{:S(2)}, u32[]{:S(2)}) %collective-permute-start.18) | collective-permute-done | bytes 524320 | tf_op jit(solution)/shard_map/ppermute | solution.py:559
  152.0 1.1 convert_add_fusion
  153.1 1.4 shard_map.127
  (89 shorter events, 7.9 us)
Async XLA Ops:
  0.6 15.2 %collective-permute-start.3 = (bf16[128,2048]{1,0:T(8,128)(2,1)}, bf16[128,2048]{1,0:T(8,128)(2,1)S(1)}, u32[]{:S(2)}, u32[]{:S(2)}) collective-permute-start(bf16[128,2048]{1,0:T(8,128)(2,1)} %bitcast.13), channel_id=1, source_target_pairs={{4,0},{5,1},{8,4},{9,5},{12,8},{13,9},{14,12},{15,13},{10,14},{11,... | collective-permute-start | bytes 1572872 | tf_op jit(solution)/shard_map/ppermute | solution.py:482
  3.7 21.6 %collective-permute-start.1 = (bf16[128,2048]{1,0:T(8,128)(2,1)}, bf16[128,2048]{1,0:T(8,128)(2,1)}, u32[]{:S(2)}, u32[]{:S(2)}) collective-permute-start(bf16[128,2048]{1,0:T(8,128)(2,1)} %bitcast.14), channel_id=1, source_target_pairs={{0,4},{1,5},{4,8},{5,9},{8,12},{9,13},{12,14},{13,15},{14,10},{15,... | collective-permute-start | bytes 1572872 | tf_op jit(solution)/shard_map/ppermute | solution.py:481
  15.9 14.9 %collective-permute-start.7 = (bf16[128,2048]{1,0:T(8,128)(2,1)S(1)}, bf16[128,2048]{1,0:T(8,128)(2,1)}, u32[]{:S(2)}, u32[]{:S(2)}) collective-permute-start(bf16[128,2048]{1,0:T(8,128)(2,1)S(1)} %collective-permute-done.3.refs_2_.refs_4_), channel_id=1, source_target_pairs={{4,0},{5,1},{8,4},{9,5},{12,8},{13,9},{14,12},{15,13},{10,14},{11,... | collective-permute-start | bytes 1572872 | tf_op jit(solution)/shard_map/ppermute | solution.py:482
  17.6 44.3 %copy-start.4 = (bf16[1,128,2048]{2,1,0:T(8,128)(2,1)S(1)}, bf16[1,128,2048]{2,1,0:T(8,128)(2,1)}, u32[]{:S(2)}) copy-start(bf16[1,128,2048]{2,1,0:T(8,128)(2,1)} %param.11) | copy-start | bytes 1572868
  17.6 72.9 %copy-start = (bf16[9,2,256,256]{3,2,1,0:T(8,128)(2,1)S(1)}, bf16[9,2,256,256]{3,2,1,0:T(8,128)(2,1)}, u32[]{:S(2)}) copy-start(bf16[9,2,256,256]{3,2,1,0:T(8,128)(2,1)} %constant.12.clone.table_ref.refs_12_) | copy-start | bytes 7077892
  20.2 80.6 %all-to-all-start = ((bf16[16,2,128,128]{3,2,1,0:T(8,128)(2,1)}), bf16[16,2,128,128]{3,2,1,0:T(8,128)(2,1)}, u32[]{:S(2)}, u32[]{:S(2)}) async-start(bf16[16,2,128,128]{3,2,1,0:T(8,128)(2,1)} %shard_map.123), calls=%async_computation | async-start | bytes 2097152 | tf_op jit(solution)/shard_map/all_to_all | solution.py:454
  25.3 29.4 %collective-permute-start.5 = (bf16[128,2048]{1,0:T(8,128)(2,1)}, bf16[128,2048]{1,0:T(8,128)(2,1)}, u32[]{:S(2)}, u32[]{:S(2)}) collective-permute-start(bf16[128,2048]{1,0:T(8,128)(2,1)} %collective-permute-done.1.refs_0_.refs_2_), channel_id=1, source_target_pairs={{0,4},{1,5},{4,8},{5,9},{8,12},{9,13},{12,14},{13,15},{14,10},{15,... | collective-permute-start | bytes 1572872 | tf_op jit(solution)/shard_map/ppermute | solution.py:481
  30.8 31.5 %collective-permute-start.11 = (bf16[128,2048]{1,0:T(8,128)(2,1)}, bf16[128,2048]{1,0:T(8,128)(2,1)S(1)}, u32[]{:S(2)}, u32[]{:S(2)}) collective-permute-start(bf16[128,2048]{1,0:T(8,128)(2,1)} %collective-permute-done.7.refs_2_.refs_8_), channel_id=1, source_target_pairs={{4,0},{5,1},{8,4},{9,5},{12,8},{13,9},{14,12},{15,13},{10,14},{11,... | collective-permute-start | bytes 1572872 | tf_op jit(solution)/shard_map/ppermute | solution.py:482
  54.7 18.4 %collective-permute-start.9 = (bf16[128,2048]{1,0:T(8,128)(2,1)}, bf16[128,2048]{1,0:T(8,128)(2,1)}, u32[]{:S(2)}, u32[]{:S(2)}) collective-permute-start(bf16[128,2048]{1,0:T(8,128)(2,1)} %collective-permute-done.5.refs_0_.refs_6_), channel_id=1, source_target_pairs={{0,4},{1,5},{4,8},{5,9},{8,12},{9,13},{12,14},{13,15},{14,10},{15,... | collective-permute-start | bytes 1572872 | tf_op jit(solution)/shard_map/ppermute | solution.py:481
  61.8 13.6 %collective-permute-start = (bf16[128,2048]{1,0:T(8,128)(2,1)S(1)}, bf16[128,2048]{1,0:T(8,128)(2,1)S(1)}, u32[]{:S(2)}, u32[]{:S(2)}) collective-permute-start(bf16[128,2048]{1,0:T(8,128)(2,1)S(1)} %bitcast.15), channel_id=1, source_target_pairs={{0,1},{1,0},{2,3},{3,2},{4,5},{5,4},{6,7},{7,6},{8,9},{9,8},{10,11... | collective-permute-start | bytes 1572872 | tf_op jit(solution)/shard_map/ppermute | solution.py:451
  61.8 18.4 %collective-permute-start.4 = (bf16[128,2048]{1,0:T(8,128)(2,1)}, bf16[128,2048]{1,0:T(8,128)(2,1)S(1)}, u32[]{:S(2)}, u32[]{:S(2)}) collective-permute-start(bf16[128,2048]{1,0:T(8,128)(2,1)} %copy-done.12), channel_id=1, source_target_pairs={{0,1},{1,0},{2,3},{3,2},{4,5},{5,4},{6,7},{7,6},{8,9},{9,8},{10,11... | collective-permute-start | bytes 1572872 | tf_op jit(solution)/shard_map/ppermute | solution.py:451
  62.3 18.7 %collective-permute-start.2 = (bf16[128,2048]{1,0:T(8,128)(2,1)}, bf16[128,2048]{1,0:T(8,128)(2,1)S(1)}, u32[]{:S(2)}, u32[]{:S(2)}) collective-permute-start(bf16[128,2048]{1,0:T(8,128)(2,1)} %collective-permute-done.1.refs_0_.refs_2_), channel_id=1, source_target_pairs={{0,1},{1,0},{2,3},{3,2},{4,5},{5,4},{6,7},{7,6},{8,9},{9,8},{10,11... | collective-permute-start | bytes 1572872 | tf_op jit(solution)/shard_map/ppermute | solution.py:451
  62.3 45.1 %copy-start.2 = (bf16[128,2048]{1,0:T(8,128)(2,1)}, bf16[128,2048]{1,0:T(8,128)(2,1)S(1)}, u32[]{:S(2)}) copy-start(bf16[128,2048]{1,0:T(8,128)(2,1)S(1)} %collective-permute-done.11.refs_2_.refs_12_) | copy-start | bytes 1572868
  62.3 19.8 %collective-permute-start.8 = (bf16[128,2048]{1,0:T(8,128)(2,1)}, bf16[128,2048]{1,0:T(8,128)(2,1)S(1)}, u32[]{:S(2)}, u32[]{:S(2)}) collective-permute-start(bf16[128,2048]{1,0:T(8,128)(2,1)} %collective-permute-done.7.refs_2_.refs_8_), channel_id=1, source_target_pairs={{0,1},{1,0},{2,3},{3,2},{4,5},{5,4},{6,7},{7,6},{8,9},{9,8},{10,11... | collective-permute-start | bytes 1572872 | tf_op jit(solution)/shard_map/ppermute | solution.py:451
  73.0 25.1 %collective-permute-start.6 = (bf16[128,2048]{1,0:T(8,128)(2,1)}, bf16[128,2048]{1,0:T(8,128)(2,1)}, u32[]{:S(2)}, u32[]{:S(2)}) collective-permute-start(bf16[128,2048]{1,0:T(8,128)(2,1)} %collective-permute-done.5.refs_0_.refs_6_), channel_id=1, source_target_pairs={{0,1},{1,0},{2,3},{3,2},{4,5},{5,4},{6,7},{7,6},{8,9},{9,8},{10,11... | collective-permute-start | bytes 1572872 | tf_op jit(solution)/shard_map/ppermute | solution.py:451
  76.2 10.6 %collective-permute-start.15 = (bf16[64,2048]{1,0:T(8,128)(2,1)}, bf16[64,2048]{1,0:T(8,128)(2,1)}, u32[]{:S(2)}, u32[]{:S(2)}) collective-permute-start(bf16[64,2048]{1,0:T(8,128)(2,1)} %slice.25), channel_id=1, source_target_pairs={{4,0},{5,1},{8,4},{9,5},{12,8},{13,9},{14,12},{15,13},{10,14},{11,... | collective-permute-start | bytes 786440 | tf_op jit(solution)/shard_map/ppermute | solution.py:486
  81.1 8.8 %collective-permute-start.13 = (bf16[64,2048]{1,0:T(8,128)(2,1)}, bf16[64,2048]{1,0:T(8,128)(2,1)}, u32[]{:S(2)}, u32[]{:S(2)}) collective-permute-start(bf16[64,2048]{1,0:T(8,128)(2,1)} %slice.24), channel_id=1, source_target_pairs={{0,4},{1,5},{4,8},{5,9},{8,12},{9,13},{12,14},{13,15},{14,10},{15,... | collective-permute-start | bytes 786440 | tf_op jit(solution)/shard_map/ppermute | solution.py:485
  81.9 25.5 %collective-permute-start.12 = (bf16[128,2048]{1,0:T(8,128)(2,1)S(1)}, bf16[128,2048]{1,0:T(8,128)(2,1)}, u32[]{:S(2)}, u32[]{:S(2)}) collective-permute-start(bf16[128,2048]{1,0:T(8,128)(2,1)S(1)} %collective-permute-done.11.refs_2_.refs_12_), channel_id=1, source_target_pairs={{0,1},{1,0},{2,3},{3,2},{4,5},{5,4},{6,7},{7,6},{8,9},{9,8},{10,11... | collective-permute-start | bytes 1572872 | tf_op jit(solution)/shard_map/ppermute | solution.py:451
  82.9 24.5 %collective-permute-start.10 = (bf16[128,2048]{1,0:T(8,128)(2,1)}, bf16[128,2048]{1,0:T(8,128)(2,1)}, u32[]{:S(2)}, u32[]{:S(2)}) collective-permute-start(bf16[128,2048]{1,0:T(8,128)(2,1)} %collective-permute-done.9.refs_0_.refs_10_), channel_id=1, source_target_pairs={{0,1},{1,0},{2,3},{3,2},{4,5},{5,4},{6,7},{7,6},{8,9},{9,8},{10,11... | collective-permute-start | bytes 1572872 | tf_op jit(solution)/shard_map/ppermute | solution.py:451
  86.8 23.4 %collective-permute-start.16 = (bf16[64,2048]{1,0:T(8,128)(2,1)}, bf16[64,2048]{1,0:T(8,128)(2,1)}, u32[]{:S(2)}, u32[]{:S(2)}) collective-permute-start(bf16[64,2048]{1,0:T(8,128)(2,1)} %collective-permute-done.15.refs_6_.refs_2_), channel_id=1, source_target_pairs={{0,1},{1,0},{2,3},{3,2},{4,5},{5,4},{6,7},{7,6},{8,9},{9,8},{10,11... | collective-permute-start | bytes 786440 | tf_op jit(solution)/shard_map/ppermute | solution.py:451
  89.8 20.4 %collective-permute-start.14 = (bf16[64,2048]{1,0:T(8,128)(2,1)}, bf16[64,2048]{1,0:T(8,128)(2,1)}, u32[]{:S(2)}, u32[]{:S(2)}) collective-permute-start(bf16[64,2048]{1,0:T(8,128)(2,1)} %collective-permute-done.13.refs_4_.refs_0_), channel_id=1, source_target_pairs={{0,1},{1,0},{2,3},{3,2},{4,5},{5,4},{6,7},{7,6},{8,9},{9,8},{10,11... | collective-permute-start | bytes 786440 | tf_op jit(solution)/shard_map/ppermute | solution.py:451
  118.2 34.9 %all-to-all-start.1 = ((bf16[16,2,128,128]{3,2,1,0:T(8,128)(2,1)}), bf16[16,2,128,128]{3,2,1,0:T(8,128)(2,1)S(1)}, u32[]{:S(2)}, u32[]{:S(2)}) async-start(bf16[16,2,128,128]{3,2,1,0:T(8,128)(2,1)} %get-tuple-element.14), calls=%async_computation.1 | async-start | bytes 2097152 | tf_op jit(solution)/shard_map/all_to_all | solution.py:454
  122.1 6.0 %copy-start.3 = (bf16[128,2048]{1,0:T(8,128)(2,1)S(1)}, bf16[128,2048]{1,0:T(8,128)(2,1)}, u32[]{:S(2)}) copy-start(bf16[128,2048]{1,0:T(8,128)(2,1)} %copy-done.2) | copy-start | bytes 1572868
  122.1 6.0 %copy-start.6 = (bf16[1,128,2048]{2,1,0:T(8,128)(2,1)S(1)}, bf16[1,128,2048]{2,1,0:T(8,128)(2,1)}, u32[]{:S(2)}) copy-start(bf16[1,128,2048]{2,1,0:T(8,128)(2,1)} %param.11) | copy-start | bytes 1572868
  122.1 6.0 %copy-start.9 = (bf16[128,2048]{1,0:T(8,128)(2,1)S(1)}, bf16[128,2048]{1,0:T(8,128)(2,1)}, u32[]{:S(2)}) copy-start(bf16[128,2048]{1,0:T(8,128)(2,1)} %copy-done.7) | copy-start | bytes 1572868
  122.1 6.0 %copy-start.14 = (bf16[128,2048]{1,0:T(8,128)(2,1)S(1)}, bf16[128,2048]{1,0:T(8,128)(2,1)}, u32[]{:S(2)}) copy-start(bf16[128,2048]{1,0:T(8,128)(2,1)} %copy-done.12) | copy-start | bytes 1572868
  122.1 6.0 %copy-start.17 = (bf16[128,2048]{1,0:T(8,128)(2,1)S(1)}, bf16[128,2048]{1,0:T(8,128)(2,1)}, u32[]{:S(2)}) copy-start(bf16[128,2048]{1,0:T(8,128)(2,1)} %copy-done.15) | copy-start | bytes 1572868
  122.1 6.0 %copy-start.20 = (bf16[128,2048]{1,0:T(8,128)(2,1)S(1)}, bf16[128,2048]{1,0:T(8,128)(2,1)}, u32[]{:S(2)}) copy-start(bf16[128,2048]{1,0:T(8,128)(2,1)} %copy-done.18) | copy-start | bytes 1572868
  126.4 14.9 %collective-permute-start.17 = (bf16[128,2048]{1,0:T(8,128)(2,1)S(1)}, bf16[128,2048]{1,0:T(8,128)(2,1)S(1)}, u32[]{:S(2)}, u32[]{:S(2)}) collective-permute-start(bf16[128,2048]{1,0:T(8,128)(2,1)S(1)} %shard_map.128), channel_id=1, source_target_pairs={{0,16},{16,0},{1,17},{17,1},{2,18},{18,2},{3,19},{19,3},{4,20},{20... | collective-permute-start | bytes 1572872 | tf_op jit(solution)/shard_map/ppermute | solution.py:559
  132.8 20.2 %copy-start.10 = (bf16[1,128,2048]{2,1,0:T(8,128)(2,1)S(1)}, bf16[1,128,2048]{2,1,0:T(8,128)(2,1)}, u32[]{:S(2)}) copy-start(bf16[1,128,2048]{2,1,0:T(8,128)(2,1)} %param.9) | copy-start | bytes 1572868
  132.9 20.2 %copy-start.11 = (bf16[1,128,2048]{2,1,0:T(8,128)(2,1)S(1)}, bf16[1,128,2048]{2,1,0:T(8,128)(2,1)}, u32[]{:S(2)}) copy-start(bf16[1,128,2048]{2,1,0:T(8,128)(2,1)} %param.10) | copy-start | bytes 1572868
  132.9 19.1 %collective-permute-start.18 = (bf16[128,2048]{1,0:T(8,128)(2,1)S(1)}, bf16[128,2048]{1,0:T(8,128)(2,1)S(1)}, u32[]{:S(2)}, u32[]{:S(2)}) collective-permute-start(bf16[128,2048]{1,0:T(8,128)(2,1)S(1)} %shard_map.130), channel_id=1, source_target_pairs={{0,16},{16,0},{1,17},{17,1},{2,18},{18,2},{3,19},{19,3},{4,20},{20... | collective-permute-start | bytes 1572872 | tf_op jit(solution)/shard_map/ppermute | solution.py:559
  (19 other events, 63.4 us)
where the time goes:
time: 155 us
  waiting for transfers between devices  72.3 us (47%)
  Pallas kernels  39.6 us (26%)
  starting transfers between devices  32 us (21%)
  local copies, waits for them, and re-layouts  7.35 us (5%)
  other arithmetic  2.2 us (1%)
    ppermute x3, waiting for transfers between devices, per_device(): ahead = lax.ppermute(ahead, 'ctx', forward)  32.5 us
    ppermute x2, waiting for transfers between devices, over_dp(): return total + lax.ppermute(x, 'dp', [(0, 1), (1, 0)]).astype(f32)  17.4 us
    ppermute x3, waiting for transfers between devices, per_device(): behind = lax.ppermute(behind, 'ctx', backward)  15.7 us
    ppermute x3, starting transfers between devices, per_device(): ahead = lax.ppermute(ahead, 'ctx', forward)  9.2 us
    pallas_call x4, Pallas kernels, grad_of(): call(functools.partial(grad_kernel, n), pltpu.HBM((n * local_t, chan), bf...  9 us
    all_to_all x2, starting transfers between devices, exchange(): return lax.all_to_all(x, 'ctx', 0, 0, tiled=True)  8.88 us
    pallas_call x1, Pallas kernels, per_device(): call(functools.partial(tail_kernel, len(parts), len(final)), (blocks, spe...  7.05 us
    pallas_call x1, Pallas kernels, per_device(): call(conv_kernel, (chan_bf, chan_bf, spec), 3, [zs, zs, zs, top, top, sem...  6.44 us
  transfers between devices with their start and end apart: 21, of which 8 were waited for; matrix products, arithmetic and copies ran while one was open for 3% of the time, Pallas kernels for 20%

commit v1 on v0

--- a/solution.py
+++ b/solution.py
@@ -202,11 +202,10 @@
 
 
 def conv_kernel(
-    got_ref,
+    mixed_ref,
     filters_ref,
     table_ref,
     conv_ref,
-    gated_ref,
     saved_ref,
     filt_ref,
     spec_ref,
@@ -216,16 +215,10 @@
     sems,
     sem,
 ):
-    local_t = got_ref.shape[2]
     fetch = pltpu.make_async_copy(filters_ref, filt_ref, sem)
     fetch.start()
-
-    def load(kind, token):
-        here = pl.ds(pl.multiple_of(token % local_t, ROWS), ROWS)
-        return got_ref[token // local_t, kind, here].astype(f32)
-
     copies = spectrum(
-        lambda n1, start: load(0, n1 * INNER + start),
+        lambda n1, start: mixed_ref[pl.ds(n1 * INNER + start, ROWS)].astype(f32),
         table_ref,
         spec_ref,
         top_ref,
@@ -235,11 +228,7 @@
     fetch.wait()
 
     def store(n1, start, value):
-        rows = pl.ds(n1 * INNER + start, ROWS)
-        value = value.astype(bf16)
-        conv_ref[rows] = value
-        query = load(1, n1 * INNER + start)
-        gated_ref[rows] = (query * value.astype(f32)).astype(bf16)
+        conv_ref[pl.ds(n1 * INNER + start, ROWS)] = value.astype(bf16)
 
     product_inverse(filt_ref, spec_ref, False, table_ref, z_ref, top_ref, bot_ref, store)
     for copy in copies:
@@ -254,13 +243,13 @@
     out_ref[...] = dot(rows_ref[...], weight_ref[...], ((1,), (1,))).astype(bf16)
 
 
-def split_kernel(key_ref, value_ref, query_ref, out_ref):
-    n, _, _, chan = out_ref.shape
+def split_kernel(key_ref, value_ref, query_ref, mixed_ref, out_ref):
+    n, _, chan = out_ref.shape
     for p in range(n):
         cols = slice(p * chan, (p + 1) * chan)
         mixed = key_ref[:, cols].astype(f32) * value_ref[:, cols].astype(f32)
-        out_ref[p, 0] = mixed.astype(bf16)
-        out_ref[p, 1] = query_ref[:, cols]
+        mixed_ref[p] = mixed.astype(bf16)
+        out_ref[p] = query_ref[:, cols]
 
 
 def finish_kernel(got_ref, key_ref, value_ref, grad_query_ref, grad_key_ref, grad_value_ref):
@@ -276,7 +265,7 @@
 def tail_kernel(n_parts, n_chunks, where_ref, *refs):
     part_refs, refs = refs[:n_parts], refs[n_parts:]
     chunk_refs, refs = refs[:n_chunks], refs[n_chunks:]
-    weight_ref, got_ref, conv_ref, filters_ref, table_ref, *refs = refs
+    weight_ref, query_ref, conv_ref, filters_ref, table_ref, *refs = refs
     out_ref, saved_ref, scaled_ref, rows_ref, grad_ref, *refs = refs
     filt_ref, spec_ref, z_ref, top_ref, bot_ref, sems, sem = refs
     fetch = pltpu.make_async_copy(filters_ref, filt_ref, sem)
@@ -290,7 +279,7 @@
     def scale(grad, unit):
         block, start = unit // halves, pl.multiple_of(unit % halves * rows, rows)
         here, place = pl.ds(start, rows), pl.ds(pl.multiple_of(unit * rows, rows), rows)
-        query = got_ref[block, 1, here].astype(f32)
+        query = query_ref[place].astype(f32)
         scaled_ref[place] = (grad * query).astype(bf16)
         out_ref[block, 0, here] = (grad * conv_ref[place].astype(f32)).astype(bf16)
 
@@ -345,14 +334,16 @@
 
 def weight_kernel(n_chunks, first, unit, where_ref, *refs):
     chunk_refs, rest = refs[:n_chunks], refs[n_chunks:]
-    gated_ref, rest = rest[0], rest[1:]
+    query_ref, conv_ref, *rest = rest
     if not first:
         sum_ref, rest = rest[0], rest[1:]
     (out_ref,) = rest
     gated, i = [], 0
     for ref in chunk_refs:
         for _ in range(ref.shape[0] // unit):
-            gated.append(gated_ref[pl.ds(pl.multiple_of(where_ref[i] * unit, unit), unit)])
+            place = pl.ds(pl.multiple_of(where_ref[i] * unit, unit), unit)
+            wide = query_ref[place].astype(f32) * conv_ref[place].astype(f32)
+            gated.append(wide.astype(bf16))
             i += 1
     left = jnp.concatenate(gated, axis=0)
     width = chunk_refs[0].shape[1]
@@ -467,10 +458,12 @@
         return [(x, offset, 0, halves), (to_partner(x), offset, 1, halves)]
 
     blocks = pltpu.HBM((size, 2, local_t, chan), bf16)
-    send = call(split_kernel, blocks, 3, flops=seq_len * chan)(
+    block = pltpu.HBM((size, local_t, chan), bf16)
+    mixed, query = call(split_kernel, (block, block), 3, flops=seq_len * chan)(
         in_hbm(key_rows), in_hbm(value_rows), in_hbm(queries_rows)
     )
-    got = exchange(send)
+    mixed = exchange(mixed).reshape(seq_len, chan)
+    query = exchange(query).reshape(seq_len, chan)
     filt_spec = call(filter_kernel, spec, 2, [zs, turned, top, top, sems], flops=one, saved=0)(
         in_hbm(filters), table
     )
@@ -485,29 +478,37 @@
     ahead = lax.ppermute(ahead[:half], "ctx", forward)
     behind = lax.ppermute(behind[half:], "ctx", backward)
     parts.append(grad_of(groups[-1]))
-    conv_chan, gated_chan, mix_spec = call(
+    conv_chan, mix_spec = call(
         conv_kernel,
-        (chan_bf, chan_bf, spec),
+        (chan_bf, spec),
         3,
         [zs, zs, zs, top, top, sems, sem],
         flops=2 * one,
         kept=(1,),
-        saved=2,
-    )(got, in_hbm(filt_spec), table)
+        saved=1,
+    )(mixed, in_hbm(filt_spec), table)
     groups.append(pair(ahead, -steps, (0,)) + pair(behind, -steps, (1,)))
 
     where = [[2 * p + h for p in sources(g[1], g[2])] for group in groups for g in group for h in g[3]]
     where = jnp.asarray(np.array(where, np.int32).T)[me]
 
-    first = [g[0] for group in groups[:-1] for g in group]
+    def weight_of(members, total, dtype):
+        pieces = [g[0] for i in members for g in groups[i]]
+        before = sum(len(g[3]) for i in range(members[0]) for g in groups[i])
+        units = sum(len(g[3]) for i in members for g in groups[i])
+        first = total is None
+        return call(
+            functools.partial(weight_kernel, len(pieces), first, half),
+            jax.ShapeDtypeStruct((chan, width), dtype),
+            len(pieces) + 2 + (not first),
+            scalars=1,
+            flops=2 * units * half * width * chan,
+        )(where[before : before + units], *pieces, query, conv_chan, *(() if first else (total,)))
+
+    total = weight_of(range(steps - 1), None, f32)
+    total = weight_of([steps - 1], total, f32)
+    part_weight = weight_of([steps], total, bf16)
     final = [g[0] for g in groups[-1]]
-    total = call(
-        functools.partial(weight_kernel, len(first), True, half),
-        pltpu.VMEM((chan, width), f32),
-        len(first) + 1,
-        scalars=1,
-        flops=2 * len(first) * local_t * width * chan,
-    )(where[: -len(final)], *first, gated_chan)
 
     back, grad_spec = call(
         functools.partial(tail_kernel, len(parts), len(final)),
@@ -529,16 +530,9 @@
         flops=2 * one,
         kept=(len(parts) + len(final) + 3,),
         saved=1,
-    )(where, *parts, *final, out_weight, got, conv_chan, in_hbm(filt_spec), table)
+    )(where, *parts, *final, out_weight, query, conv_chan, in_hbm(filt_spec), table)
     back = exchange(back)
 
-    part_weight = call(
-        functools.partial(weight_kernel, len(final), False, half),
-        jax.ShapeDtypeStruct((chan, width), bf16),
-        len(final) + 2,
-        scalars=1,
-        flops=2 * len(final) * half * width * chan,
-    )(where[-len(final) :], *final, gated_chan, total)
     taps = call(
         taps_kernel,
         jax.ShapeDtypeStruct((chan, seq_len), bf16),

time: 155 us -> 150 us (0.968)
  waiting for transfers between devices: 72.3 us -> 59.9 us
  starting transfers between devices: 32 us -> 36.3 us
  Pallas kernels: 39.6 us -> 42.2 us
    ppermute x3, waiting for transfers between devices: 32.5 us -> 18.4 us  [per_device(): ahead = lax.ppermute(ahead, 'ctx', forward)]
    all_to_all x2 -> x3, starting transfers between devices: 8.88 us -> 15.5 us  [exchange(): return lax.all_to_all(x, 'ctx', 0, 0, tiled=True)]
    ppermute x1, waiting for transfers between devices: 3 us -> 6.06 us  [per_device(): ahead = lax.ppermute(ahead[:half], 'ctx', forward)]
    ppermute x3, starting transfers between devices: 9.2 us -> 6.53 us  [per_device(): ahead = lax.ppermute(ahead, 'ctx', forward)]
    ppermute x2, waiting for transfers between devices: 17.4 us -> 15.2 us  [over_dp(): return total + lax.ppermute(x, 'dp', [(0, 1), (1, 0)]).astype(f32)]
    pallas_call x4, Pallas kernels: 9 us -> 10.9 us  [grad_of(): call(functools.partial(grad_kernel, n), pltpu.HBM((n * local_t, chan), bf...]
    unnamed x60 -> x24, local copies, waits for them, and re-layouts: 4.17 us -> 3.72 us
    pallas_call x4 -> x5, Pallas kernels: 13.8 us -> 13.7 us  [the longest x3 6.91 us: weight_of(): call(functools.partial(weight_kernel, len(pieces), first, half), jax.Shap...]
  transfers between devices with their start and end apart: 21 -> 22, of which waited for: 8 -> 8; matrix products, arithmetic and copies ran while one was open for 3% -> 4% of each run, Pallas kernels for 20% -> 22%
where the time goes in v1:
time: 150 us; the launch traced here: 149 us
  waiting for transfers between devices  59.9 us (40%)
  Pallas kernels  42.2 us (28%)
  starting transfers between devices  36.3 us (24%)
  local copies, waits for them, and re-layouts  7.89 us (5%)
  other arithmetic  2.2 us (1%)
    ppermute x3, waiting for transfers between devices, per_device(): ahead = lax.ppermute(ahead, 'ctx', forward)  18.4 us
    ppermute x3, waiting for transfers between devices, per_device(): behind = lax.ppermute(behind, 'ctx', backward)  16.5 us
    all_to_all x3, starting transfers between devices, exchange(): return lax.all_to_all(x, 'ctx', 0, 0, tiled=True)  15.5 us
    ppermute x2, waiting for transfers between devices, over_dp(): return total + lax.ppermute(x, 'dp', [(0, 1), (1, 0)]).astype(f32)  15.2 us
    pallas_call x4, Pallas kernels, grad_of(): call(functools.partial(grad_kernel, n), pltpu.HBM((n * local_t, chan), bf...  10.9 us
    pallas_call x3, Pallas kernels, weight_of(): call(functools.partial(weight_kernel, len(pieces), first, half), jax.Shap...  6.91 us
    pallas_call x1, Pallas kernels, per_device(): call(functools.partial(tail_kernel, len(parts), len(final)), (blocks, spe...  6.76 us
    ppermute x3, starting transfers between devices, per_device(): ahead = lax.ppermute(ahead, 'ctx', forward)  6.53 us
  transfers between devices with their start and end apart: 22, of which 8 were waited for; matrix products, arithmetic and copies ran while one was open for 4% of the time, Pallas kernels for 22%

profile of v1, /device:TPU:0, one launch (start us, length us, event | category | flops | bytes accessed | tf_op | source)
XLA Modules:
  0.0 149.3 jit_solution(2301268634679079602)
XLA Ops:
  0.6 3.0 %collective-permute-start.3 = (bf16[128,2048]{1,0:T(8,128)(2,1)}, bf16[128,2048]{1,0:T(8,128)(2,1)}, u32[]{:S(2)}, u32[]{:S(2)}) collective-permute-start(bf16[128,2048]{1,0:T(8,128)(2,1)} %bitcast.1.refs_0_), channel_id=1, source_target_pairs={{4,0},{5,1},{8,4},{9,5},{12,8},{13,9},{14,12},{15,13},{10,14},{11,... | collective-permute-start | bytes 1572872 | tf_op jit(solution)/shard_map/ppermute | solution.py:475
  3.8 12.2 %collective-permute-done.3.refs_2_.refs_4_ = bf16[128,2048]{1,0:T(8,128)(2,1)} collective-permute-done((bf16[128,2048]{1,0:T(8,128)(2,1)}, bf16[128,2048]{1,0:T(8,128)(2,1)}, u32[]{:S(2)}, u32[]{:S(2)}) %collective-permute-start.3) | collective-permute-done | bytes 524320 | tf_op jit(solution)/shard_map/ppermute | solution.py:475
  16.0 1.7 %collective-permute-start.7 = (bf16[128,2048]{1,0:T(8,128)(2,1)}, bf16[128,2048]{1,0:T(8,128)(2,1)}, u32[]{:S(2)}, u32[]{:S(2)}) collective-permute-start(bf16[128,2048]{1,0:T(8,128)(2,1)} %collective-permute-done.3.refs_2_.refs_4_), channel_id=1, source_target_pairs={{4,0},{5,1},{8,4},{9,5},{12,8},{13,9},{14,12},{15,13},{10,14},{11,... | collective-permute-start | bytes 1572872 | tf_op jit(solution)/shard_map/ppermute | solution.py:475
  17.7 2.6 %shard_map.123 = (bf16[16,128,128]{2,1,0:T(8,128)(2,1)}, bf16[16,128,128]{2,1,0:T(8,128)(2,1)}) custom-call(bf16[128,2048]{1,0:T(8,128)(2,1)} %bitcast.22, bf16[128,2048]{1,0:T(8,128)(2,1)} %bitcast.24, bf16[128,2048]{1,0:T(8,128)(2,1)} %bitcast.26), custom_call_target="tpu_custom_call" | custom-call | flops 262144 | bytes 1048576 | tf_op jit(solution)/shard_map/pallas_call | solution.py:462
  20.3 5.0 %all-to-all-start.1 = ((bf16[16,128,128]{2,1,0:T(8,128)(2,1)}), bf16[16,128,128]{2,1,0:T(8,128)(2,1)S(1)}, u32[]{:S(2)}, u32[]{:S(2)}) async-start(bf16[16,128,128]{2,1,0:T(8,128)(2,1)} %get-tuple-element.15), calls=%async_computation.1 | async-start | bytes 1048576 | tf_op jit(solution)/shard_map/all_to_all | solution.py:445
  25.3 2.0 %collective-permute-start.5 = (bf16[128,2048]{1,0:T(8,128)(2,1)}, bf16[128,2048]{1,0:T(8,128)(2,1)}, u32[]{:S(2)}, u32[]{:S(2)}) collective-permute-start(bf16[128,2048]{1,0:T(8,128)(2,1)} %collective-permute-done.1.refs_0_.refs_2_), channel_id=1, source_target_pairs={{0,4},{1,5},{4,8},{5,9},{8,12},{9,13},{12,14},{13,15},{14,10},{15,... | collective-permute-start | bytes 1572872 | tf_op jit(solution)/shard_map/ppermute | solution.py:474
  27.3 4.4 %collective-permute-done.7.refs_2_.refs_8_ = bf16[128,2048]{1,0:T(8,128)(2,1)} collective-permute-done((bf16[128,2048]{1,0:T(8,128)(2,1)}, bf16[128,2048]{1,0:T(8,128)(2,1)}, u32[]{:S(2)}, u32[]{:S(2)}) %collective-permute-start.7) | collective-permute-done | bytes 524320 | tf_op jit(solution)/shard_map/ppermute | solution.py:475
  32.1 14.0 %collective-permute-done.5.refs_0_.refs_6_ = bf16[128,2048]{1,0:T(8,128)(2,1)} collective-permute-done((bf16[128,2048]{1,0:T(8,128)(2,1)}, bf16[128,2048]{1,0:T(8,128)(2,1)}, u32[]{:S(2)}, u32[]{:S(2)}) %collective-permute-start.5) | collective-permute-done | bytes 524320 | tf_op jit(solution)/shard_map/ppermute | solution.py:474
  46.2 4.4 %collective-permute-start.9 = (bf16[128,2048]{1,0:T(8,128)(2,1)}, bf16[128,2048]{1,0:T(8,128)(2,1)}, u32[]{:S(2)}, u32[]{:S(2)}) collective-permute-start(bf16[128,2048]{1,0:T(8,128)(2,1)} %collective-permute-done.5.refs_0_.refs_6_), channel_id=1, source_target_pairs={{0,4},{1,5},{4,8},{5,9},{8,12},{9,13},{12,14},{13,15},{14,10},{15,... | collective-permute-start | bytes 1572872 | tf_op jit(solution)/shard_map/ppermute | solution.py:474
  51.6 5.6 %all-to-all-start = ((bf16[16,128,128]{2,1,0:T(8,128)(2,1)}), bf16[16,128,128]{2,1,0:T(8,128)(2,1)S(1)}, u32[]{:S(2)}, u32[]{:S(2)}) async-start(bf16[16,128,128]{2,1,0:T(8,128)(2,1)} %get-tuple-element.14), calls=%async_computation | async-start | bytes 1048576 | tf_op jit(solution)/shard_map/all_to_all | solution.py:445
  57.2 1.7 %slice.33 = bf16[64,2048]{1,0:T(8,128)(2,1)} slice(bf16[128,2048]{1,0:T(8,128)(2,1)} %collective-permute-done.11.refs_2_), slice={[64:128], [0:2048]} | slice | bytes 524288 | tf_op jit(solution)/shard_map/slice | solution.py:479
  58.9 4.3 %collective-permute-done.9.refs_0_ = bf16[128,2048]{1,0:T(8,128)(2,1)} collective-permute-done((bf16[128,2048]{1,0:T(8,128)(2,1)}, bf16[128,2048]{1,0:T(8,128)(2,1)}, u32[]{:S(2)}, u32[]{:S(2)}) %collective-permute-start.9) | collective-permute-done | bytes 524320 | tf_op jit(solution)/shard_map/ppermute | solution.py:474
  63.2 5.2 %collective-permute-start.15 = (bf16[64,2048]{1,0:T(8,128)(2,1)}, bf16[64,2048]{1,0:T(8,128)(2,1)}, u32[]{:S(2)}, u32[]{:S(2)}) collective-permute-start(bf16[64,2048]{1,0:T(8,128)(2,1)} %slice.33), channel_id=1, source_target_pairs={{4,0},{5,1},{8,4},{9,5},{12,8},{13,9},{14,12},{15,13},{10,14},{11,... | collective-permute-start | bytes 786440 | tf_op jit(solution)/shard_map/ppermute | solution.py:479
  68.4 1.7 %slice.32 = bf16[64,2048]{1,0:T(8,128)(2,1)} slice(bf16[128,2048]{1,0:T(8,128)(2,1)} %collective-permute-done.9.refs_0_), slice={[0:64], [0:2048]} | slice | bytes 524288 | tf_op jit(solution)/shard_map/slice | solution.py:478
  70.8 3.7 %collective-permute-done.15.refs_6_.refs_2_ = bf16[64,2048]{1,0:T(8,128)(2,1)} collective-permute-done((bf16[64,2048]{1,0:T(8,128)(2,1)}, bf16[64,2048]{1,0:T(8,128)(2,1)}, u32[]{:S(2)}, u32[]{:S(2)}) %collective-permute-start.15) | collective-permute-done | bytes 262176 | tf_op jit(solution)/shard_map/ppermute | solution.py:479
  74.5 6.1 %collective-permute-done.13.refs_4_.refs_0_ = bf16[64,2048]{1,0:T(8,128)(2,1)} collective-permute-done((bf16[64,2048]{1,0:T(8,128)(2,1)}, bf16[64,2048]{1,0:T(8,128)(2,1)}, u32[]{:S(2)}, u32[]{:S(2)}) %collective-permute-start.13) | collective-permute-done | bytes 262176 | tf_op jit(solution)/shard_map/ppermute | solution.py:478
  81.2 4.0 %shard_map.124.filters_ref.refs_11_ = f32[9,256,256]{2,1,0:T(8,128)} custom-call(f32[128,2048]{1,0:T(8,128)} %filters_ref.1, bf16[9,2,256,256]{3,2,1,0:T(8,128)(2,1)S(1)} %copy-done), custom_call_target="tpu_custom_call" | custom-call | flops 603979776 | bytes 1048576 | tf_op jit(solution)/shard_map/pallas_call | solution.py:467
  85.3 2.3 %shard_map.119.refs_0_ = bf16[256,128]{1,0:T(8,128)(2,1)} custom-call(bf16[128,2048]{1,0:T(8,128)(2,1)} %bitcast.1.refs_0_, bf16[128,2048]{1,0:T(8,128)(2,1)} %collective-permute-done.refs_1_, bf16[128,2048]{1,0:T(8,128)(2,1)S(1)} %copy-done.1), custom_call_target="tpu_custom_call" | custom-call | flops 134217728 | bytes 1048576 | tf_op jit(solution)/shard_map/pallas_call | solution.py:449
  87.5 4.1 %shard_map.125 = (bf16[2048,128]{1,0:T(8,128)(2,1)}, f32[9,256,256]{2,1,0:T(8,128)}) custom-call(bf16[2048,128]{1,0:T(8,128)(2,1)S(1)} %bitcast.21, f32[9,256,256]{2,1,0:T(8,128)} %shard_map.124.filters_ref.refs_11_, bf16[9,2,256,256]{3,2,1,0:T(8,128)(2,1)S(1)} %copy-done), custom_call_target="tpu_custom_call" | custom-call | flops 1207959552 | bytes 1048576 | tf_op jit(solution)/shard_map/pallas_call | solution.py:481
  91.6 2.9 %shard_map.120.refs_1_ = bf16[512,128]{1,0:T(8,128)(2,1)} custom-call(bf16[128,2048]{1,0:T(8,128)(2,1)} %collective-permute-done.1.refs_0_.refs_2_, bf16[128,2048]{1,0:T(8,128)(2,1)} %collective-permute-done.2.refs_1_.refs_3_, bf16[128,2048]{1,0:T(8,128)(2,1)} %collective-permute-done.3.refs_2_.refs_4_, ...), custom_call_target="tpu_custom_call" | custom-call | flops 268435456 | bytes 1048576 | tf_op jit(solution)/shard_map/pallas_call | solution.py:449
  94.5 2.9 %shard_map.121.refs_2_ = bf16[512,128]{1,0:T(8,128)(2,1)} custom-call(bf16[128,2048]{1,0:T(8,128)(2,1)} %collective-permute-done.5.refs_0_.refs_6_, bf16[128,2048]{1,0:T(8,128)(2,1)} %collective-permute-done.6.refs_1_.refs_7_, bf16[128,2048]{1,0:T(8,128)(2,1)} %collective-permute-done.7.refs_2_.refs_8_, ...), custom_call_target="tpu_custom_call" | custom-call | flops 268435456 | bytes 1048576 | tf_op jit(solution)/shard_map/pallas_call | solution.py:449
  97.4 2.9 %shard_map.122.refs_3_ = bf16[512,128]{1,0:T(8,128)(2,1)} custom-call(bf16[128,2048]{1,0:T(8,128)(2,1)} %collective-permute-done.9.refs_0_, bf16[128,2048]{1,0:T(8,128)(2,1)} %collective-permute-done.10.refs_1_, bf16[128,2048]{1,0:T(8,128)(2,1)} %collective-permute-done.11.refs_2_, bf16[128,2048]{1,0:T(8,128)(2,1)} %collective-permute-done.12.refs_3_, ...), custom_call_target="tpu_custom_call" | custom-call | flops 268435456 | bytes 1048576 | tf_op jit(solution)/shard_map/pallas_call | solution.py:449
  104.0 6.8 %shard_map.126 = (bf16[16,2,128,128]{3,2,1,0:T(8,128)(2,1)}, f32[9,256,256]{2,1,0:T(8,128)}) custom-call(s32[32]{0:T(128)S(1)} %get-tuple-element.24.where_ref, bf16[256,128]{1,0:T(8,128)(2,1)S(1)} %copy-done.11, bf16[512,128]{1,0:T(8,128)(2,1)S(1)} %copy-done.8, bf16[512,128]{1,0:T(8,128)(2,1)S(1)} %copy-done.9, bf16[512,128]{1,0:T(8,128)(2,1)S(1)} %copy-done.10, ...), custom_call_target="tpu_custom_call" | custom-call | flops 1207959552 | bytes 1048576 | tf_op jit(solution)/shard_map/pallas_call | solution.py:513
  110.8 5.0 %all-to-all-start.2 = ((bf16[16,2,128,128]{3,2,1,0:T(8,128)(2,1)}), bf16[16,2,128,128]{3,2,1,0:T(8,128)(2,1)}, u32[]{:S(2)}, u32[]{:S(2)}) async-start(bf16[16,2,128,128]{3,2,1,0:T(8,128)(2,1)} %get-tuple-element.17), calls=%async_computation.2 | async-start | bytes 2097152 | tf_op jit(solution)/shard_map/all_to_all | solution.py:445
  115.9 4.2 %shard_map.128 = bf16[128,2048]{1,0:T(8,128)(2,1)S(1)} custom-call(f32[9,256,256]{2,1,0:T(8,128)} %get-tuple-element.21.saved_mix, f32[9,256,256]{2,1,0:T(8,128)} %get-tuple-element.22.saved_grad, bf16[9,2,256,256]{3,2,1,0:T(8,128)(2,1)S(1)} %copy-done), custom_call_target="tpu_custom_call" | custom-call | flops 603979776 | bytes 1048576 | tf_op jit(solution)/shard_map/pallas_call | solution.py:536
  120.1 1.6 %collective-permute-start.17 = (bf16[128,2048]{1,0:T(8,128)(2,1)S(1)}, bf16[128,2048]{1,0:T(8,128)(2,1)S(1)}, u32[]{:S(2)}, u32[]{:S(2)}) collective-permute-start(bf16[128,2048]{1,0:T(8,128)(2,1)S(1)} %shard_map.128), channel_id=1, source_target_pairs={{0,16},{16,0},{1,17},{17,1},{2,18},{18,2},{3,19},{19,3},{4,20},{20... | collective-permute-start | bytes 1572872 | tf_op jit(solution)/shard_map/ppermute | solution.py:553
  121.7 3.4 %shard_map.129.refs_6_ = f32[128,2048]{1,0:T(8,128)S(1)} custom-call(s32[20]{0:T(128)S(1)} %slice_bitcast_fusion.where_ref, bf16[128,2048]{1,0:T(8,128)(2,1)} %bitcast.1.refs_0_, bf16[128,2048]{1,0:T(8,128)(2,1)} %collective-permute-done.refs_1_, bf16[128,2048]{1,0:T(8,128)(2,1)} %collective-permute-done.1.refs_0_.refs_2_, ...), custom_call_target="tpu_custom_call" | custom-call | flops 671088640 | bytes 1048576 | tf_op jit(solution)/shard_map/pallas_call | solution.py:500
  125.1 2.0 %shard_map.130.refs_6_ = f32[128,2048]{1,0:T(8,128)S(1)} custom-call(s32[8]{0:T(128)S(1)} %slice_bitcast_fusion.1.where_ref, bf16[128,2048]{1,0:T(8,128)(2,1)} %collective-permute-done.9.refs_0_, bf16[128,2048]{1,0:T(8,128)(2,1)} %collective-permute-done.10.refs_1_, bf16[128,2048]{1,0:T(8,128)(2,1)} %collective-permute-done.11.refs_2_, ...), custom_call_target="tpu_custom_call" | custom-call | flops 268435456 | bytes 1048576 | tf_op jit(solution)/shard_map/pallas_call | solution.py:500
  127.1 1.5 %shard_map.131 = bf16[128,2048]{1,0:T(8,128)(2,1)S(1)} custom-call(s32[4]{0:T(128)S(1)} %slice_bitcast_fusion.2.where_ref, bf16[64,2048]{1,0:T(8,128)(2,1)} %collective-permute-done.13.refs_4_.refs_0_, bf16[64,2048]{1,0:T(8,128)(2,1)} %collective-permute-done.14.refs_5_.refs_1_, bf16[64,2048]{1,0:T(8,128)(2,1)} %collective-permute-done.15.refs_6_.refs_2_, ...), custom_call_target="tpu_custom_call" | custom-call | flops 134217728 | bytes 1048576 | tf_op jit(solution)/shard_map/pallas_call | solution.py:500
  129.3 5.7 %collective-permute-done.17 = bf16[128,2048]{1,0:T(8,128)(2,1)S(1)} collective-permute-done((bf16[128,2048]{1,0:T(8,128)(2,1)S(1)}, bf16[128,2048]{1,0:T(8,128)(2,1)S(1)}, u32[]{:S(2)}, u32[]{:S(2)}) %collective-permute-start.17) | collective-permute-done | bytes 524320 | tf_op jit(solution)/shard_map/ppermute | solution.py:553
  136.0 9.5 %collective-permute-done.18 = bf16[128,2048]{1,0:T(8,128)(2,1)S(1)} collective-permute-done((bf16[128,2048]{1,0:T(8,128)(2,1)S(1)}, bf16[128,2048]{1,0:T(8,128)(2,1)S(1)}, u32[]{:S(2)}, u32[]{:S(2)}) %collective-permute-start.18) | collective-permute-done | bytes 524320 | tf_op jit(solution)/shard_map/ppermute | solution.py:553
  146.6 2.6 %shard_map.127 = (bf16[128,2048]{1,0:T(8,128)(2,1)}, bf16[128,2048]{1,0:T(8,128)(2,1)}, bf16[128,2048]{1,0:T(8,128)(2,1)}) custom-call(bf16[16,2,128,128]{3,2,1,0:T(8,128)(2,1)} %all-to-all-done.2.got_ref, bf16[128,2048]{1,0:T(8,128)(2,1)S(1)} %bitcast.23, bf16[128,2048]{1,0:T(8,128)(2,1)S(1)} %bitcast.25), custom_call_target="tpu_custom_call" | custom-call | flops 262144 | bytes 1048576 | tf_op jit(solution)/shard_map/pallas_call | solution.py:545
  (57 shorter events, 9.7 us)
Async XLA Ops:
  0.6 15.3 %collective-permute-start.3 = (bf16[128,2048]{1,0:T(8,128)(2,1)}, bf16[128,2048]{1,0:T(8,128)(2,1)}, u32[]{:S(2)}, u32[]{:S(2)}) collective-permute-start(bf16[128,2048]{1,0:T(8,128)(2,1)} %bitcast.1.refs_0_), channel_id=1, source_target_pairs={{4,0},{5,1},{8,4},{9,5},{12,8},{13,9},{14,12},{15,13},{10,14},{11,... | collective-permute-start | bytes 1572872 | tf_op jit(solution)/shard_map/ppermute | solution.py:475
  3.7 21.6 %collective-permute-start.1 = (bf16[128,2048]{1,0:T(8,128)(2,1)}, bf16[128,2048]{1,0:T(8,128)(2,1)}, u32[]{:S(2)}, u32[]{:S(2)}) collective-permute-start(bf16[128,2048]{1,0:T(8,128)(2,1)} %bitcast.1.refs_0_), channel_id=1, source_target_pairs={{0,4},{1,5},{4,8},{5,9},{8,12},{9,13},{12,14},{13,15},{14,10},{15,... | collective-permute-start | bytes 1572872 | tf_op jit(solution)/shard_map/ppermute | solution.py:474
  16.0 15.7 %collective-permute-start.7 = (bf16[128,2048]{1,0:T(8,128)(2,1)}, bf16[128,2048]{1,0:T(8,128)(2,1)}, u32[]{:S(2)}, u32[]{:S(2)}) collective-permute-start(bf16[128,2048]{1,0:T(8,128)(2,1)} %collective-permute-done.3.refs_2_.refs_4_), channel_id=1, source_target_pairs={{4,0},{5,1},{8,4},{9,5},{12,8},{13,9},{14,12},{15,13},{10,14},{11,... | collective-permute-start | bytes 1572872 | tf_op jit(solution)/shard_map/ppermute | solution.py:475
  17.7 63.6 %copy-start = (bf16[9,2,256,256]{3,2,1,0:T(8,128)(2,1)S(1)}, bf16[9,2,256,256]{3,2,1,0:T(8,128)(2,1)}, u32[]{:S(2)}) copy-start(bf16[9,2,256,256]{3,2,1,0:T(8,128)(2,1)} %constant.12.clone.table_ref.refs_12_) | copy-start | bytes 7077892
  20.3 31.3 %all-to-all-start.1 = ((bf16[16,128,128]{2,1,0:T(8,128)(2,1)}), bf16[16,128,128]{2,1,0:T(8,128)(2,1)S(1)}, u32[]{:S(2)}, u32[]{:S(2)}) async-start(bf16[16,128,128]{2,1,0:T(8,128)(2,1)} %get-tuple-element.15), calls=%async_computation.1 | async-start | bytes 1048576 | tf_op jit(solution)/shard_map/all_to_all | solution.py:445
  25.3 20.9 %collective-permute-start.5 = (bf16[128,2048]{1,0:T(8,128)(2,1)}, bf16[128,2048]{1,0:T(8,128)(2,1)}, u32[]{:S(2)}, u32[]{:S(2)}) collective-permute-start(bf16[128,2048]{1,0:T(8,128)(2,1)} %collective-permute-done.1.refs_0_.refs_2_), channel_id=1, source_target_pairs={{0,4},{1,5},{4,8},{5,9},{8,12},{9,13},{12,14},{13,15},{14,10},{15,... | collective-permute-start | bytes 1572872 | tf_op jit(solution)/shard_map/ppermute | solution.py:474
  31.6 19.5 %collective-permute-start.11 = (bf16[128,2048]{1,0:T(8,128)(2,1)}, bf16[128,2048]{1,0:T(8,128)(2,1)}, u32[]{:S(2)}, u32[]{:S(2)}) collective-permute-start(bf16[128,2048]{1,0:T(8,128)(2,1)} %collective-permute-done.7.refs_2_.refs_8_), channel_id=1, source_target_pairs={{4,0},{5,1},{8,4},{9,5},{12,8},{13,9},{14,12},{15,13},{10,14},{11,... | collective-permute-start | bytes 1572872 | tf_op jit(solution)/shard_map/ppermute | solution.py:475
  46.2 17.1 %collective-permute-start.9 = (bf16[128,2048]{1,0:T(8,128)(2,1)}, bf16[128,2048]{1,0:T(8,128)(2,1)}, u32[]{:S(2)}, u32[]{:S(2)}) collective-permute-start(bf16[128,2048]{1,0:T(8,128)(2,1)} %collective-permute-done.5.refs_0_.refs_6_), channel_id=1, source_target_pairs={{0,4},{1,5},{4,8},{5,9},{8,12},{9,13},{12,14},{13,15},{14,10},{15,... | collective-permute-start | bytes 1572872 | tf_op jit(solution)/shard_map/ppermute | solution.py:474
  50.6 19.5 %collective-permute-start = (bf16[128,2048]{1,0:T(8,128)(2,1)}, bf16[128,2048]{1,0:T(8,128)(2,1)}, u32[]{:S(2)}, u32[]{:S(2)}) collective-permute-start(bf16[128,2048]{1,0:T(8,128)(2,1)} %bitcast.1.refs_0_), channel_id=1, source_target_pairs={{0,1},{1,0},{2,3},{3,2},{4,5},{5,4},{6,7},{7,6},{8,9},{9,8},{10,11... | collective-permute-start | bytes 1572872 | tf_op jit(solution)/shard_map/ppermute | solution.py:442
  50.6 19.5 %collective-permute-start.4 = (bf16[128,2048]{1,0:T(8,128)(2,1)}, bf16[128,2048]{1,0:T(8,128)(2,1)}, u32[]{:S(2)}, u32[]{:S(2)}) collective-permute-start(bf16[128,2048]{1,0:T(8,128)(2,1)} %collective-permute-done.3.refs_2_.refs_4_), channel_id=1, source_target_pairs={{0,1},{1,0},{2,3},{3,2},{4,5},{5,4},{6,7},{7,6},{8,9},{9,8},{10,11... | collective-permute-start | bytes 1572872 | tf_op jit(solution)/shard_map/ppermute | solution.py:442
  51.1 19.1 %collective-permute-start.2 = (bf16[128,2048]{1,0:T(8,128)(2,1)}, bf16[128,2048]{1,0:T(8,128)(2,1)}, u32[]{:S(2)}, u32[]{:S(2)}) collective-permute-start(bf16[128,2048]{1,0:T(8,128)(2,1)} %collective-permute-done.1.refs_0_.refs_2_), channel_id=1, source_target_pairs={{0,1},{1,0},{2,3},{3,2},{4,5},{5,4},{6,7},{7,6},{8,9},{9,8},{10,11... | collective-permute-start | bytes 1572872 | tf_op jit(solution)/shard_map/ppermute | solution.py:442
  51.1 19.6 %collective-permute-start.8 = (bf16[128,2048]{1,0:T(8,128)(2,1)}, bf16[128,2048]{1,0:T(8,128)(2,1)}, u32[]{:S(2)}, u32[]{:S(2)}) collective-permute-start(bf16[128,2048]{1,0:T(8,128)(2,1)} %collective-permute-done.7.refs_2_.refs_8_), channel_id=1, source_target_pairs={{0,1},{1,0},{2,3},{3,2},{4,5},{5,4},{6,7},{7,6},{8,9},{9,8},{10,11... | collective-permute-start | bytes 1572872 | tf_op jit(solution)/shard_map/ppermute | solution.py:442
  51.6 28.9 %copy-start.4 = (bf16[16,128,128]{2,1,0:T(8,128)(2,1)}, bf16[16,128,128]{2,1,0:T(8,128)(2,1)S(1)}, u32[]{:S(2)}) copy-start(bf16[16,128,128]{2,1,0:T(8,128)(2,1)S(1)} %all-to-all-done.1) | copy-start | bytes 1572868
  51.6 48.7 %all-to-all-start = ((bf16[16,128,128]{2,1,0:T(8,128)(2,1)}), bf16[16,128,128]{2,1,0:T(8,128)(2,1)S(1)}, u32[]{:S(2)}, u32[]{:S(2)}) async-start(bf16[16,128,128]{2,1,0:T(8,128)(2,1)} %get-tuple-element.14), calls=%async_computation | async-start | bytes 1048576 | tf_op jit(solution)/shard_map/all_to_all | solution.py:445
  63.2 11.2 %collective-permute-start.15 = (bf16[64,2048]{1,0:T(8,128)(2,1)}, bf16[64,2048]{1,0:T(8,128)(2,1)}, u32[]{:S(2)}, u32[]{:S(2)}) collective-permute-start(bf16[64,2048]{1,0:T(8,128)(2,1)} %slice.33), channel_id=1, source_target_pairs={{4,0},{5,1},{8,4},{9,5},{12,8},{13,9},{14,12},{15,13},{10,14},{11,... | collective-permute-start | bytes 786440 | tf_op jit(solution)/shard_map/ppermute | solution.py:479
  70.1 10.4 %collective-permute-start.13 = (bf16[64,2048]{1,0:T(8,128)(2,1)}, bf16[64,2048]{1,0:T(8,128)(2,1)}, u32[]{:S(2)}, u32[]{:S(2)}) collective-permute-start(bf16[64,2048]{1,0:T(8,128)(2,1)} %slice.32), channel_id=1, source_target_pairs={{0,4},{1,5},{4,8},{5,9},{8,12},{9,13},{12,14},{13,15},{14,10},{15,... | collective-permute-start | bytes 786440 | tf_op jit(solution)/shard_map/ppermute | solution.py:478
  70.1 24.4 %collective-permute-start.6 = (bf16[128,2048]{1,0:T(8,128)(2,1)}, bf16[128,2048]{1,0:T(8,128)(2,1)}, u32[]{:S(2)}, u32[]{:S(2)}) collective-permute-start(bf16[128,2048]{1,0:T(8,128)(2,1)} %collective-permute-done.5.refs_0_.refs_6_), channel_id=1, source_target_pairs={{0,1},{1,0},{2,3},{3,2},{4,5},{5,4},{6,7},{7,6},{8,9},{9,8},{10,11... | collective-permute-start | bytes 1572872 | tf_op jit(solution)/shard_map/ppermute | solution.py:442
  70.2 27.3 %collective-permute-start.12 = (bf16[128,2048]{1,0:T(8,128)(2,1)}, bf16[128,2048]{1,0:T(8,128)(2,1)}, u32[]{:S(2)}, u32[]{:S(2)}) collective-permute-start(bf16[128,2048]{1,0:T(8,128)(2,1)} %collective-permute-done.11.refs_2_), channel_id=1, source_target_pairs={{0,1},{1,0},{2,3},{3,2},{4,5},{5,4},{6,7},{7,6},{8,9},{9,8},{10,11... | collective-permute-start | bytes 1572872 | tf_op jit(solution)/shard_map/ppermute | solution.py:442
  70.7 26.8 %collective-permute-start.10 = (bf16[128,2048]{1,0:T(8,128)(2,1)}, bf16[128,2048]{1,0:T(8,128)(2,1)}, u32[]{:S(2)}, u32[]{:S(2)}) collective-permute-start(bf16[128,2048]{1,0:T(8,128)(2,1)} %collective-permute-done.9.refs_0_), channel_id=1, source_target_pairs={{0,1},{1,0},{2,3},{3,2},{4,5},{5,4},{6,7},{7,6},{8,9},{9,8},{10,11... | collective-permute-start | bytes 1572872 | tf_op jit(solution)/shard_map/ppermute | solution.py:442
  74.5 25.9 %collective-permute-start.16 = (bf16[64,2048]{1,0:T(8,128)(2,1)}, bf16[64,2048]{1,0:T(8,128)(2,1)}, u32[]{:S(2)}, u32[]{:S(2)}) collective-permute-start(bf16[64,2048]{1,0:T(8,128)(2,1)} %collective-permute-done.15.refs_6_.refs_2_), channel_id=1, source_target_pairs={{0,1},{1,0},{2,3},{3,2},{4,5},{5,4},{6,7},{7,6},{8,9},{9,8},{10,11... | collective-permute-start | bytes 786440 | tf_op jit(solution)/shard_map/ppermute | solution.py:442
  80.5 19.8 %collective-permute-start.14 = (bf16[64,2048]{1,0:T(8,128)(2,1)}, bf16[64,2048]{1,0:T(8,128)(2,1)}, u32[]{:S(2)}, u32[]{:S(2)}) collective-permute-start(bf16[64,2048]{1,0:T(8,128)(2,1)} %collective-permute-done.13.refs_4_.refs_0_), channel_id=1, source_target_pairs={{0,1},{1,0},{2,3},{3,2},{4,5},{5,4},{6,7},{7,6},{8,9},{9,8},{10,11... | collective-permute-start | bytes 786440 | tf_op jit(solution)/shard_map/ppermute | solution.py:442
  81.2 4.0 %copy-start.1 = (bf16[128,2048]{1,0:T(8,128)(2,1)S(1)}, bf16[128,2048]{1,0:T(8,128)(2,1)}, u32[]{:S(2)}) copy-start(bf16[128,2048]{1,0:T(8,128)(2,1)} %refs_8_.1) | copy-start | bytes 1572868
  81.2 6.3 %copy-start.5 = (bf16[16,128,128]{2,1,0:T(8,128)(2,1)S(1)}, bf16[16,128,128]{2,1,0:T(8,128)(2,1)}, u32[]{:S(2)}) copy-start(bf16[16,128,128]{2,1,0:T(8,128)(2,1)} %copy-done.4) | copy-start | bytes 1572868
  94.5 5.8 %copy-start.8 = (bf16[512,128]{1,0:T(8,128)(2,1)S(1)}, bf16[512,128]{1,0:T(8,128)(2,1)}, u32[]{:S(2)}) copy-start(bf16[512,128]{1,0:T(8,128)(2,1)} %shard_map.120.refs_1_) | copy-start | bytes 393220
  100.3 1.0 copy-start.2
  101.4 0.9 copy-start.9
  110.8 35.8 %all-to-all-start.2 = ((bf16[16,2,128,128]{3,2,1,0:T(8,128)(2,1)}), bf16[16,2,128,128]{3,2,1,0:T(8,128)(2,1)}, u32[]{:S(2)}, u32[]{:S(2)}) async-start(bf16[16,2,128,128]{3,2,1,0:T(8,128)(2,1)} %get-tuple-element.17), calls=%async_computation.2 | async-start | bytes 2097152 | tf_op jit(solution)/shard_map/all_to_all | solution.py:445
  115.9 5.8 %copy-start.3 = (bf16[2048,128]{1,0:T(8,128)(2,1)S(1)}, bf16[2048,128]{1,0:T(8,128)(2,1)}, u32[]{:S(2)}) copy-start(bf16[2048,128]{1,0:T(8,128)(2,1)} %get-tuple-element.16.refs_10_.refs_11_.refs_5_) | copy-start | bytes 1572868
  120.1 14.9 %collective-permute-start.17 = (bf16[128,2048]{1,0:T(8,128)(2,1)S(1)}, bf16[128,2048]{1,0:T(8,128)(2,1)S(1)}, u32[]{:S(2)}, u32[]{:S(2)}) collective-permute-start(bf16[128,2048]{1,0:T(8,128)(2,1)S(1)} %shard_map.128), channel_id=1, source_target_pairs={{0,16},{16,0},{1,17},{17,1},{2,18},{18,2},{3,19},{19,3},{4,20},{20... | collective-permute-start | bytes 1572872 | tf_op jit(solution)/shard_map/ppermute | solution.py:553
  128.6 18.0 %copy-start.6 = (bf16[1,128,2048]{2,1,0:T(8,128)(2,1)S(1)}, bf16[1,128,2048]{2,1,0:T(8,128)(2,1)}, u32[]{:S(2)}) copy-start(bf16[1,128,2048]{2,1,0:T(8,128)(2,1)} %param.9) | copy-start | bytes 1572868
  128.6 18.0 %copy-start.7 = (bf16[1,128,2048]{2,1,0:T(8,128)(2,1)S(1)}, bf16[1,128,2048]{2,1,0:T(8,128)(2,1)}, u32[]{:S(2)}) copy-start(bf16[1,128,2048]{2,1,0:T(8,128)(2,1)} %param.10) | copy-start | bytes 1572868
  128.7 16.9 %collective-permute-start.18 = (bf16[128,2048]{1,0:T(8,128)(2,1)S(1)}, bf16[128,2048]{1,0:T(8,128)(2,1)S(1)}, u32[]{:S(2)}, u32[]{:S(2)}) collective-permute-start(bf16[128,2048]{1,0:T(8,128)(2,1)S(1)} %shard_map.131), channel_id=1, source_target_pairs={{0,16},{16,0},{1,17},{17,1},{2,18},{18,2},{3,19},{19,3},{4,20},{20... | collective-permute-start | bytes 1572872 | tf_op jit(solution)/shard_map/ppermute | solution.py:553
  (2 other events, 1.7 us)

commit v2 on v1

--- a/solution.py
+++ b/solution.py
@@ -11,7 +11,7 @@
 
 
 INNER = 256
-ROWS = 16
+ROWS = 32
 VMEM_LIMIT = 20 << 20
 f32 = jnp.float32
 bf16 = jnp.bfloat16
@@ -240,16 +240,29 @@
     rows = chunk_refs[0].shape[0]
     for i, ref in enumerate(chunk_refs):
         rows_ref[i * rows : (i + 1) * rows] = ref[...]
-    out_ref[...] = dot(rows_ref[...], weight_ref[...], ((1,), (1,))).astype(bf16)
-
-
-def split_kernel(key_ref, value_ref, query_ref, mixed_ref, out_ref):
+    out_ref[...] = dot(rows_ref[...], weight_ref[...]).astype(bf16)
+
+
+def turn_kernel(in_ref, out_ref):
+    out_ref[...] = in_ref[...].astype(f32).T.astype(bf16)
+
+
+def mix_kernel(key_ref, value_ref, out_ref):
     n, _, chan = out_ref.shape
     for p in range(n):
         cols = slice(p * chan, (p + 1) * chan)
         mixed = key_ref[:, cols].astype(f32) * value_ref[:, cols].astype(f32)
-        mixed_ref[p] = mixed.astype(bf16)
-        out_ref[p] = query_ref[:, cols]
+        out_ref[p] = mixed.astype(bf16)
+
+
+def split_kernel(in_ref, out_ref):
+    n, _, chan = out_ref.shape
+    for p in range(n):
+        out_ref[p] = in_ref[:, p * chan : (p + 1) * chan]
+
+
+def cut_kernel(start, in_ref, out_ref):
+    out_ref[...] = in_ref[start : start + out_ref.shape[0]]
 
 
 def finish_kernel(got_ref, key_ref, value_ref, grad_query_ref, grad_key_ref, grad_value_ref):
@@ -289,7 +302,7 @@
             i += 1
     for j, ref in enumerate(chunk_refs):
         rows_ref[j * rows : (j + 1) * rows] = ref[...]
-    grad_ref[...] = dot(rows_ref[...], weight, ((1,), (1,))).astype(bf16)
+    grad_ref[...] = dot(rows_ref[...], weight).astype(bf16)
     for j in range(n_chunks):
         scale(grad_ref[j * rows : (j + 1) * rows].astype(f32), where_ref[i + j])
     copies = spectrum(
@@ -441,6 +454,10 @@
     def to_partner(x):
         return lax.ppermute(x, "ctx", partner)
 
+    def cut(x, start):
+        out = jax.ShapeDtypeStruct((half, width), bf16)
+        return call(functools.partial(cut_kernel, start), out, 1, flops=half * width)(x)
+
     def exchange(x):
         return lax.all_to_all(x, "ctx", 0, 0, tiled=True)
 
@@ -452,16 +469,18 @@
             n + 1,
             [pltpu.VMEM((n * local_t, width), bf16)],
             flops=2 * n * local_t * width * chan,
-        )(*[g[0] for g in group], out_weight)
+        )(*[g[0] for g in group], turned_weight)
 
     def pair(x, offset, halves=(0, 1)):
         return [(x, offset, 0, halves), (to_partner(x), offset, 1, halves)]
 
+    turned_weight = call(
+        turn_kernel, jax.ShapeDtypeStruct((width, chan), bf16), 1, flops=width * chan
+    )(out_weight)
     blocks = pltpu.HBM((size, 2, local_t, chan), bf16)
     block = pltpu.HBM((size, local_t, chan), bf16)
-    mixed, query = call(split_kernel, (block, block), 3, flops=seq_len * chan)(
-        in_hbm(key_rows), in_hbm(value_rows), in_hbm(queries_rows)
-    )
+    mixed = call(mix_kernel, block, 2, flops=seq_len * chan)(in_hbm(key_rows), in_hbm(value_rows))
+    query = call(split_kernel, block, 1, flops=seq_len * chan)(in_hbm(queries_rows))
     mixed = exchange(mixed).reshape(seq_len, chan)
     query = exchange(query).reshape(seq_len, chan)
     filt_spec = call(filter_kernel, spec, 2, [zs, turned, top, top, sems], flops=one, saved=0)(
@@ -475,8 +494,8 @@
         behind = lax.ppermute(behind, "ctx", backward)
         groups.append(pair(ahead, -step) + pair(behind, step))
         parts.append(grad_of(groups[step - 1]))
-    ahead = lax.ppermute(ahead[:half], "ctx", forward)
-    behind = lax.ppermute(behind[half:], "ctx", backward)
+    ahead = lax.ppermute(cut(ahead, 0), "ctx", forward)
+    behind = lax.ppermute(cut(behind, half), "ctx", backward)
     parts.append(grad_of(groups[-1]))
     conv_chan, mix_spec = call(
         conv_kernel,
@@ -530,7 +549,7 @@
         flops=2 * one,
         kept=(len(parts) + len(final) + 3,),
         saved=1,
-    )(where, *parts, *final, out_weight, query, conv_chan, in_hbm(filt_spec), table)
+    )(where, *parts, *final, turned_weight, query, conv_chan, in_hbm(filt_spec), table)
     back = exchange(back)
 
     taps = call(

time: 150 us -> 150 us (level)
  Pallas kernels: 42.2 us -> 46.7 us
  waiting for transfers between devices: 59.9 us -> 57.5 us
  local copies, waits for them, and re-layouts: 7.89 us -> 5.6 us
    pallas_call x1 -> x5, Pallas kernels: 2.64 us -> 7.91 us  [the longest x2 3.52 us: cut(): call(functools.partial(cut_kernel, start), out, 1, flops=half * width)(x)]
    ppermute x3, waiting for transfers between devices: 18.4 us -> 14.7 us  [per_device(): ahead = lax.ppermute(ahead, 'ctx', forward)]
    slice x2 -> x0, local copies, waits for them, and re-layouts: 3.34 us -> none  [the longest x1 1.67 us: per_device(): behind = lax.ppermute(behind[half:], 'ctx', backward)]
  transfers between devices with their start and end apart: 22 -> 22, of which waited for: 8 -> 8; matrix products, arithmetic and copies ran while one was open for 4% -> 2% of each run, Pallas kernels for 22% -> 25%
where the time goes in v2:
time: 150 us; the launch traced here: 149 us
  waiting for transfers between devices  57.5 us (38%)
  Pallas kernels  46.7 us (31%)
  starting transfers between devices  36.4 us (24%)
  local copies, waits for them, and re-layouts  5.6 us (4%)
  other arithmetic  2.2 us (1%)
    ppermute x3, waiting for transfers between devices, per_device(): behind = lax.ppermute(behind, 'ctx', backward)  17.6 us
    all_to_all x3, starting transfers between devices, exchange(): return lax.all_to_all(x, 'ctx', 0, 0, tiled=True)  15.8 us
    ppermute x2, waiting for transfers between devices, over_dp(): return total + lax.ppermute(x, 'dp', [(0, 1), (1, 0)]).astype(f32)  15.2 us
    ppermute x3, waiting for transfers between devices, per_device(): ahead = lax.ppermute(ahead, 'ctx', forward)  14.7 us
    pallas_call x4, Pallas kernels, grad_of(): call(functools.partial(grad_kernel, n), pltpu.HBM((n * local_t, chan), bf...  10.9 us
    pallas_call x3, Pallas kernels, weight_of(): call(functools.partial(weight_kernel, len(pieces), first, half), jax.Shap...  6.91 us
    ppermute x3, starting transfers between devices, per_device(): ahead = lax.ppermute(ahead, 'ctx', forward)  6.53 us
    ppermute x1, waiting for transfers between devices, per_device(): behind = lax.ppermute(cut(behind, half), 'ctx', backward)  6.22 us
  transfers between devices with their start and end apart: 22, of which 8 were waited for; matrix products, arithmetic and copies ran while one was open for 2% of the time, Pallas kernels for 25%

profile of v2, /device:TPU:0, one launch (start us, length us, event | category | flops | bytes accessed | tf_op | source)
XLA Modules:
  0.0 149.2 jit_solution(12526999352414368879)
XLA Ops:
  0.6 3.0 %collective-permute-start.3 = (bf16[128,2048]{1,0:T(8,128)(2,1)}, bf16[128,2048]{1,0:T(8,128)(2,1)}, u32[]{:S(2)}, u32[]{:S(2)}) collective-permute-start(bf16[128,2048]{1,0:T(8,128)(2,1)} %bitcast.1.refs_0_), channel_id=1, source_target_pairs={{4,0},{5,1},{8,4},{9,5},{12,8},{13,9},{14,12},{15,13},{10,14},{11,... | collective-permute-start | bytes 1572872 | tf_op jit(solution)/shard_map/ppermute | solution.py:494
  3.8 12.2 %collective-permute-done.3.refs_2_.refs_4_ = bf16[128,2048]{1,0:T(8,128)(2,1)} collective-permute-done((bf16[128,2048]{1,0:T(8,128)(2,1)}, bf16[128,2048]{1,0:T(8,128)(2,1)}, u32[]{:S(2)}, u32[]{:S(2)}) %collective-permute-start.3) | collective-permute-done | bytes 524320 | tf_op jit(solution)/shard_map/ppermute | solution.py:494
  16.0 1.7 %collective-permute-start.7 = (bf16[128,2048]{1,0:T(8,128)(2,1)}, bf16[128,2048]{1,0:T(8,128)(2,1)}, u32[]{:S(2)}, u32[]{:S(2)}) collective-permute-start(bf16[128,2048]{1,0:T(8,128)(2,1)} %collective-permute-done.3.refs_2_.refs_4_), channel_id=1, source_target_pairs={{4,0},{5,1},{8,4},{9,5},{12,8},{13,9},{14,12},{15,13},{10,14},{11,... | collective-permute-start | bytes 1572872 | tf_op jit(solution)/shard_map/ppermute | solution.py:494
  17.7 2.1 %shard_map.127 = bf16[16,128,128]{2,1,0:T(8,128)(2,1)} custom-call(bf16[128,2048]{1,0:T(8,128)(2,1)} %bitcast.22, bf16[128,2048]{1,0:T(8,128)(2,1)} %bitcast.24), custom_call_target="tpu_custom_call" | custom-call | flops 262144 | bytes 1048576 | tf_op jit(solution)/shard_map/pallas_call | solution.py:482
  19.8 5.0 %all-to-all-start.1 = ((bf16[16,128,128]{2,1,0:T(8,128)(2,1)}), bf16[16,128,128]{2,1,0:T(8,128)(2,1)S(1)}, u32[]{:S(2)}, u32[]{:S(2)}) async-start(bf16[16,128,128]{2,1,0:T(8,128)(2,1)} %shard_map.127), calls=%async_computation.1 | async-start | bytes 1048576 | tf_op jit(solution)/shard_map/all_to_all | solution.py:462
  24.8 2.0 %collective-permute-start.5 = (bf16[128,2048]{1,0:T(8,128)(2,1)}, bf16[128,2048]{1,0:T(8,128)(2,1)}, u32[]{:S(2)}, u32[]{:S(2)}) collective-permute-start(bf16[128,2048]{1,0:T(8,128)(2,1)} %collective-permute-done.1.refs_0_.refs_2_), channel_id=1, source_target_pairs={{0,4},{1,5},{4,8},{5,9},{8,12},{9,13},{12,14},{13,15},{14,10},{15,... | collective-permute-start | bytes 1572872 | tf_op jit(solution)/shard_map/ppermute | solution.py:493
  26.8 5.4 %collective-permute-done.7.refs_2_.refs_8_ = bf16[128,2048]{1,0:T(8,128)(2,1)} collective-permute-done((bf16[128,2048]{1,0:T(8,128)(2,1)}, bf16[128,2048]{1,0:T(8,128)(2,1)}, u32[]{:S(2)}, u32[]{:S(2)}) %collective-permute-start.7) | collective-permute-done | bytes 524320 | tf_op jit(solution)/shard_map/ppermute | solution.py:494
  32.8 12.8 %collective-permute-done.5.refs_0_.refs_6_ = bf16[128,2048]{1,0:T(8,128)(2,1)} collective-permute-done((bf16[128,2048]{1,0:T(8,128)(2,1)}, bf16[128,2048]{1,0:T(8,128)(2,1)}, u32[]{:S(2)}, u32[]{:S(2)}) %collective-permute-start.5) | collective-permute-done | bytes 524320 | tf_op jit(solution)/shard_map/ppermute | solution.py:493
  45.6 4.4 %collective-permute-start.9 = (bf16[128,2048]{1,0:T(8,128)(2,1)}, bf16[128,2048]{1,0:T(8,128)(2,1)}, u32[]{:S(2)}, u32[]{:S(2)}) collective-permute-start(bf16[128,2048]{1,0:T(8,128)(2,1)} %collective-permute-done.5.refs_0_.refs_6_), channel_id=1, source_target_pairs={{0,4},{1,5},{4,8},{5,9},{8,12},{9,13},{12,14},{13,15},{14,10},{15,... | collective-permute-start | bytes 1572872 | tf_op jit(solution)/shard_map/ppermute | solution.py:493
  51.1 2.1 %shard_map.126 = bf16[16,128,128]{2,1,0:T(8,128)(2,1)} custom-call(bf16[128,2048]{1,0:T(8,128)(2,1)} %bitcast.26), custom_call_target="tpu_custom_call" | custom-call | flops 262144 | bytes 1048576 | tf_op jit(solution)/shard_map/pallas_call | solution.py:483
  53.2 5.7 %all-to-all-start = ((bf16[16,128,128]{2,1,0:T(8,128)(2,1)}), bf16[16,128,128]{2,1,0:T(8,128)(2,1)S(1)}, u32[]{:S(2)}, u32[]{:S(2)}) async-start(bf16[16,128,128]{2,1,0:T(8,128)(2,1)} %shard_map.126), calls=%async_computation | async-start | bytes 1048576 | tf_op jit(solution)/shard_map/all_to_all | solution.py:462
  58.9 1.8 %shard_map.125 = bf16[64,2048]{1,0:T(8,128)(2,1)} custom-call(bf16[128,2048]{1,0:T(8,128)(2,1)} %collective-permute-done.11.refs_2_.in_ref), custom_call_target="tpu_custom_call" | custom-call | flops 131072 | bytes 1048576 | tf_op jit(solution)/shard_map/pallas_call | solution.py:459
  60.6 1.9 %collective-permute-done.9.refs_0_.in_ref = bf16[128,2048]{1,0:T(8,128)(2,1)} collective-permute-done((bf16[128,2048]{1,0:T(8,128)(2,1)}, bf16[128,2048]{1,0:T(8,128)(2,1)}, u32[]{:S(2)}, u32[]{:S(2)}) %collective-permute-start.9) | collective-permute-done | bytes 524320 | tf_op jit(solution)/shard_map/ppermute | solution.py:493
  62.5 4.9 %collective-permute-start.15 = (bf16[64,2048]{1,0:T(8,128)(2,1)}, bf16[64,2048]{1,0:T(8,128)(2,1)}, u32[]{:S(2)}, u32[]{:S(2)}) collective-permute-start(bf16[64,2048]{1,0:T(8,128)(2,1)} %shard_map.125), channel_id=1, source_target_pairs={{4,0},{5,1},{8,4},{9,5},{12,8},{13,9},{14,12},{15,13},{10,14},{11,... | collective-permute-start | bytes 786440 | tf_op jit(solution)/shard_map/ppermute | solution.py:498
  67.5 1.8 %shard_map.124 = bf16[64,2048]{1,0:T(8,128)(2,1)} custom-call(bf16[128,2048]{1,0:T(8,128)(2,1)} %collective-permute-done.9.refs_0_.in_ref), custom_call_target="tpu_custom_call" | custom-call | flops 131072 | bytes 1048576 | tf_op jit(solution)/shard_map/pallas_call | solution.py:459
  69.9 6.2 %collective-permute-done.15.refs_6_.refs_2_ = bf16[64,2048]{1,0:T(8,128)(2,1)} collective-permute-done((bf16[64,2048]{1,0:T(8,128)(2,1)}, bf16[64,2048]{1,0:T(8,128)(2,1)}, u32[]{:S(2)}, u32[]{:S(2)}) %collective-permute-start.15) | collective-permute-done | bytes 262176 | tf_op jit(solution)/shard_map/ppermute | solution.py:498
  76.1 3.7 %collective-permute-done.13.refs_4_.refs_0_ = bf16[64,2048]{1,0:T(8,128)(2,1)} collective-permute-done((bf16[64,2048]{1,0:T(8,128)(2,1)}, bf16[64,2048]{1,0:T(8,128)(2,1)}, u32[]{:S(2)}, u32[]{:S(2)}) %collective-permute-start.13) | collective-permute-done | bytes 262176 | tf_op jit(solution)/shard_map/ppermute | solution.py:497
  81.8 4.0 %shard_map.128.filters_ref.refs_11_ = f32[9,256,256]{2,1,0:T(8,128)} custom-call(f32[128,2048]{1,0:T(8,128)} %filters_ref.1, bf16[9,2,256,256]{3,2,1,0:T(8,128)(2,1)S(1)} %copy-done), custom_call_target="tpu_custom_call" | custom-call | flops 603979776 | bytes 1048576 | tf_op jit(solution)/shard_map/pallas_call | solution.py:486
  85.8 2.2 %shard_map.120.refs_0_ = bf16[256,128]{1,0:T(8,128)(2,1)} custom-call(bf16[128,2048]{1,0:T(8,128)(2,1)} %bitcast.1.refs_0_, bf16[128,2048]{1,0:T(8,128)(2,1)} %collective-permute-done.refs_1_, bf16[2048,128]{1,0:T(8,128)(2,1)S(1)} %shard_map.119.refs_2_.refs_4_.refs_8_), custom_call_target="tpu_custom_call" | custom-call | flops 134217728 | bytes 1048576 | tf_op jit(solution)/shard_map/pallas_call | solution.py:466
  88.0 4.0 %shard_map.129 = (bf16[2048,128]{1,0:T(8,128)(2,1)}, f32[9,256,256]{2,1,0:T(8,128)}) custom-call(bf16[2048,128]{1,0:T(8,128)(2,1)S(1)} %bitcast.21, f32[9,256,256]{2,1,0:T(8,128)} %shard_map.128.filters_ref.refs_11_, bf16[9,2,256,256]{3,2,1,0:T(8,128)(2,1)S(1)} %copy-done), custom_call_target="tpu_custom_call" | custom-call | flops 1207959552 | bytes 1048576 | tf_op jit(solution)/shard_map/pallas_call | solution.py:500
  92.1 2.9 %shard_map.121.refs_1_ = bf16[512,128]{1,0:T(8,128)(2,1)} custom-call(bf16[128,2048]{1,0:T(8,128)(2,1)} %collective-permute-done.1.refs_0_.refs_2_, bf16[128,2048]{1,0:T(8,128)(2,1)} %collective-permute-done.2.refs_1_.refs_3_, bf16[128,2048]{1,0:T(8,128)(2,1)} %collective-permute-done.3.refs_2_.refs_4_, ...), custom_call_target="tpu_custom_call" | custom-call | flops 268435456 | bytes 1048576 | tf_op jit(solution)/shard_map/pallas_call | solution.py:466
  95.0 2.9 %shard_map.122.refs_2_ = bf16[512,128]{1,0:T(8,128)(2,1)} custom-call(bf16[128,2048]{1,0:T(8,128)(2,1)} %collective-permute-done.5.refs_0_.refs_6_, bf16[128,2048]{1,0:T(8,128)(2,1)} %collective-permute-done.6.refs_1_.refs_7_, bf16[128,2048]{1,0:T(8,128)(2,1)} %collective-permute-done.7.refs_2_.refs_8_, ...), custom_call_target="tpu_custom_call" | custom-call | flops 268435456 | bytes 1048576 | tf_op jit(solution)/shard_map/pallas_call | solution.py:466
  97.9 2.9 %shard_map.123.refs_3_ = bf16[512,128]{1,0:T(8,128)(2,1)} custom-call(bf16[128,2048]{1,0:T(8,128)(2,1)} %collective-permute-done.9.refs_0_.in_ref, bf16[128,2048]{1,0:T(8,128)(2,1)} %collective-permute-done.10.refs_1_, bf16[128,2048]{1,0:T(8,128)(2,1)} %collective-permute-done.11.refs_2_.in_ref, bf16[128,2048]{1,0:T(8,128)(2,1)} %collective-permute-done.12.refs_3_, ...), custom_call_target="tpu_custom_call" | custom-call | flops 268435456 | bytes 1048576 | tf_op jit(solution)/shard_map/pallas_call | solution.py:466
  104.5 6.1 %shard_map.130 = (bf16[16,2,128,128]{3,2,1,0:T(8,128)(2,1)}, f32[9,256,256]{2,1,0:T(8,128)}) custom-call(s32[32]{0:T(128)S(1)} %get-tuple-element.20.where_ref, bf16[256,128]{1,0:T(8,128)(2,1)S(1)} %copy-done.11, bf16[512,128]{1,0:T(8,128)(2,1)S(1)} %copy-done.7, bf16[512,128]{1,0:T(8,128)(2,1)S(1)} %copy-done.8, bf16[512,128]{1,0:T(8,128)(2,1)S(1)} %copy-done.9, ...), custom_call_target="tpu_custom_call" | custom-call | flops 1207959552 | bytes 1048576 | tf_op jit(solution)/shard_map/pallas_call | solution.py:532
  110.6 5.1 %all-to-all-start.2 = ((bf16[16,2,128,128]{3,2,1,0:T(8,128)(2,1)}), bf16[16,2,128,128]{3,2,1,0:T(8,128)(2,1)}, u32[]{:S(2)}, u32[]{:S(2)}) async-start(bf16[16,2,128,128]{3,2,1,0:T(8,128)(2,1)} %get-tuple-element.13), calls=%async_computation.2 | async-start | bytes 2097152 | tf_op jit(solution)/shard_map/all_to_all | solution.py:462
  115.8 4.2 %shard_map.132 = bf16[128,2048]{1,0:T(8,128)(2,1)S(1)} custom-call(f32[9,256,256]{2,1,0:T(8,128)} %get-tuple-element.17.saved_mix, f32[9,256,256]{2,1,0:T(8,128)} %get-tuple-element.18.saved_grad, bf16[9,2,256,256]{3,2,1,0:T(8,128)(2,1)S(1)} %copy-done), custom_call_target="tpu_custom_call" | custom-call | flops 603979776 | bytes 1048576 | tf_op jit(solution)/shard_map/pallas_call | solution.py:555
  120.0 1.6 %collective-permute-start.17 = (bf16[128,2048]{1,0:T(8,128)(2,1)S(1)}, bf16[128,2048]{1,0:T(8,128)(2,1)S(1)}, u32[]{:S(2)}, u32[]{:S(2)}) collective-permute-start(bf16[128,2048]{1,0:T(8,128)(2,1)S(1)} %shard_map.132), channel_id=1, source_target_pairs={{0,16},{16,0},{1,17},{17,1},{2,18},{18,2},{3,19},{19,3},{4,20},{20... | collective-permute-start | bytes 1572872 | tf_op jit(solution)/shard_map/ppermute | solution.py:572
  121.6 3.4 %shard_map.133.refs_6_ = f32[128,2048]{1,0:T(8,128)S(1)} custom-call(s32[20]{0:T(128)S(1)} %slice_bitcast_fusion.where_ref, bf16[128,2048]{1,0:T(8,128)(2,1)} %bitcast.1.refs_0_, bf16[128,2048]{1,0:T(8,128)(2,1)} %collective-permute-done.refs_1_, bf16[128,2048]{1,0:T(8,128)(2,1)} %collective-permute-done.1.refs_0_.refs_2_, ...), custom_call_target="tpu_custom_call" | custom-call | flops 671088640 | bytes 1048576 | tf_op jit(solution)/shard_map/pallas_call | solution.py:519
  125.0 2.0 %shard_map.134.refs_6_ = f32[128,2048]{1,0:T(8,128)S(1)} custom-call(s32[8]{0:T(128)S(1)} %slice_bitcast_fusion.1.where_ref, bf16[128,2048]{1,0:T(8,128)(2,1)} %collective-permute-done.9.refs_0_.in_ref, bf16[128,2048]{1,0:T(8,128)(2,1)} %collective-permute-done.10.refs_1_, bf16[128,2048]{1,0:T(8,128)(2,1)} %collective-permute-done.11.refs_2_.in_ref, ...), custom_call_target="tpu_custom_call" | custom-call | flops 268435456 | bytes 1048576 | tf_op jit(solution)/shard_map/pallas_call | solution.py:519
  129.2 5.7 %collective-permute-done.17 = bf16[128,2048]{1,0:T(8,128)(2,1)S(1)} collective-permute-done((bf16[128,2048]{1,0:T(8,128)(2,1)S(1)}, bf16[128,2048]{1,0:T(8,128)(2,1)S(1)}, u32[]{:S(2)}, u32[]{:S(2)}) %collective-permute-start.17) | collective-permute-done | bytes 524320 | tf_op jit(solution)/shard_map/ppermute | solution.py:572
  135.9 9.5 %collective-permute-done.18 = bf16[128,2048]{1,0:T(8,128)(2,1)S(1)} collective-permute-done((bf16[128,2048]{1,0:T(8,128)(2,1)S(1)}, bf16[128,2048]{1,0:T(8,128)(2,1)S(1)}, u32[]{:S(2)}, u32[]{:S(2)}) %collective-permute-start.18) | collective-permute-done | bytes 524320 | tf_op jit(solution)/shard_map/ppermute | solution.py:572
  146.6 2.6 %shard_map.131 = (bf16[128,2048]{1,0:T(8,128)(2,1)}, bf16[128,2048]{1,0:T(8,128)(2,1)}, bf16[128,2048]{1,0:T(8,128)(2,1)}) custom-call(bf16[16,2,128,128]{3,2,1,0:T(8,128)(2,1)} %all-to-all-done.2.got_ref, bf16[128,2048]{1,0:T(8,128)(2,1)S(1)} %bitcast.23, bf16[128,2048]{1,0:T(8,128)(2,1)S(1)} %bitcast.25), custom_call_target="tpu_custom_call" | custom-call | flops 262144 | bytes 1048576 | tf_op jit(solution)/shard_map/pallas_call | solution.py:564
  (59 shorter events, 12.6 us)
Async XLA Ops:
  0.6 15.3 %collective-permute-start.3 = (bf16[128,2048]{1,0:T(8,128)(2,1)}, bf16[128,2048]{1,0:T(8,128)(2,1)}, u32[]{:S(2)}, u32[]{:S(2)}) collective-permute-start(bf16[128,2048]{1,0:T(8,128)(2,1)} %bitcast.1.refs_0_), channel_id=1, source_target_pairs={{4,0},{5,1},{8,4},{9,5},{12,8},{13,9},{14,12},{15,13},{10,14},{11,... | collective-permute-start | bytes 1572872 | tf_op jit(solution)/shard_map/ppermute | solution.py:494
  3.7 21.1 %collective-permute-start.1 = (bf16[128,2048]{1,0:T(8,128)(2,1)}, bf16[128,2048]{1,0:T(8,128)(2,1)}, u32[]{:S(2)}, u32[]{:S(2)}) collective-permute-start(bf16[128,2048]{1,0:T(8,128)(2,1)} %bitcast.1.refs_0_), channel_id=1, source_target_pairs={{0,4},{1,5},{4,8},{5,9},{8,12},{9,13},{12,14},{13,15},{14,10},{15,... | collective-permute-start | bytes 1572872 | tf_op jit(solution)/shard_map/ppermute | solution.py:493
  16.0 16.2 %collective-permute-start.7 = (bf16[128,2048]{1,0:T(8,128)(2,1)}, bf16[128,2048]{1,0:T(8,128)(2,1)}, u32[]{:S(2)}, u32[]{:S(2)}) collective-permute-start(bf16[128,2048]{1,0:T(8,128)(2,1)} %collective-permute-done.3.refs_2_.refs_4_), channel_id=1, source_target_pairs={{4,0},{5,1},{8,4},{9,5},{12,8},{13,9},{14,12},{15,13},{10,14},{11,... | collective-permute-start | bytes 1572872 | tf_op jit(solution)/shard_map/ppermute | solution.py:494
  19.8 33.4 %all-to-all-start.1 = ((bf16[16,128,128]{2,1,0:T(8,128)(2,1)}), bf16[16,128,128]{2,1,0:T(8,128)(2,1)S(1)}, u32[]{:S(2)}, u32[]{:S(2)}) async-start(bf16[16,128,128]{2,1,0:T(8,128)(2,1)} %shard_map.127), calls=%async_computation.1 | async-start | bytes 1048576 | tf_op jit(solution)/shard_map/all_to_all | solution.py:462
  24.8 20.9 %collective-permute-start.5 = (bf16[128,2048]{1,0:T(8,128)(2,1)}, bf16[128,2048]{1,0:T(8,128)(2,1)}, u32[]{:S(2)}, u32[]{:S(2)}) collective-permute-start(bf16[128,2048]{1,0:T(8,128)(2,1)} %collective-permute-done.1.refs_0_.refs_2_), channel_id=1, source_target_pairs={{0,4},{1,5},{4,8},{5,9},{8,12},{9,13},{12,14},{13,15},{14,10},{15,... | collective-permute-start | bytes 1572872 | tf_op jit(solution)/shard_map/ppermute | solution.py:493
  32.2 18.4 %collective-permute-start.11 = (bf16[128,2048]{1,0:T(8,128)(2,1)}, bf16[128,2048]{1,0:T(8,128)(2,1)}, u32[]{:S(2)}, u32[]{:S(2)}) collective-permute-start(bf16[128,2048]{1,0:T(8,128)(2,1)} %collective-permute-done.7.refs_2_.refs_8_), channel_id=1, source_target_pairs={{4,0},{5,1},{8,4},{9,5},{12,8},{13,9},{14,12},{15,13},{10,14},{11,... | collective-permute-start | bytes 1572872 | tf_op jit(solution)/shard_map/ppermute | solution.py:494
  45.6 16.9 %collective-permute-start.9 = (bf16[128,2048]{1,0:T(8,128)(2,1)}, bf16[128,2048]{1,0:T(8,128)(2,1)}, u32[]{:S(2)}, u32[]{:S(2)}) collective-permute-start(bf16[128,2048]{1,0:T(8,128)(2,1)} %collective-permute-done.5.refs_0_.refs_6_), channel_id=1, source_target_pairs={{0,4},{1,5},{4,8},{5,9},{8,12},{9,13},{12,14},{13,15},{14,10},{15,... | collective-permute-start | bytes 1572872 | tf_op jit(solution)/shard_map/ppermute | solution.py:493
  50.1 19.2 %collective-permute-start = (bf16[128,2048]{1,0:T(8,128)(2,1)}, bf16[128,2048]{1,0:T(8,128)(2,1)}, u32[]{:S(2)}, u32[]{:S(2)}) collective-permute-start(bf16[128,2048]{1,0:T(8,128)(2,1)} %bitcast.1.refs_0_), channel_id=1, source_target_pairs={{0,1},{1,0},{2,3},{3,2},{4,5},{5,4},{6,7},{7,6},{8,9},{9,8},{10,11... | collective-permute-start | bytes 1572872 | tf_op jit(solution)/shard_map/ppermute | solution.py:455
  50.1 19.2 %collective-permute-start.4 = (bf16[128,2048]{1,0:T(8,128)(2,1)}, bf16[128,2048]{1,0:T(8,128)(2,1)}, u32[]{:S(2)}, u32[]{:S(2)}) collective-permute-start(bf16[128,2048]{1,0:T(8,128)(2,1)} %collective-permute-done.3.refs_2_.refs_4_), channel_id=1, source_target_pairs={{0,1},{1,0},{2,3},{3,2},{4,5},{5,4},{6,7},{7,6},{8,9},{9,8},{10,11... | collective-permute-start | bytes 1572872 | tf_op jit(solution)/shard_map/ppermute | solution.py:455
  50.6 18.7 %collective-permute-start.2 = (bf16[128,2048]{1,0:T(8,128)(2,1)}, bf16[128,2048]{1,0:T(8,128)(2,1)}, u32[]{:S(2)}, u32[]{:S(2)}) collective-permute-start(bf16[128,2048]{1,0:T(8,128)(2,1)} %collective-permute-done.1.refs_0_.refs_2_), channel_id=1, source_target_pairs={{0,1},{1,0},{2,3},{3,2},{4,5},{5,4},{6,7},{7,6},{8,9},{9,8},{10,11... | collective-permute-start | bytes 1572872 | tf_op jit(solution)/shard_map/ppermute | solution.py:455
  50.6 19.2 %collective-permute-start.8 = (bf16[128,2048]{1,0:T(8,128)(2,1)}, bf16[128,2048]{1,0:T(8,128)(2,1)}, u32[]{:S(2)}, u32[]{:S(2)}) collective-permute-start(bf16[128,2048]{1,0:T(8,128)(2,1)} %collective-permute-done.7.refs_2_.refs_8_), channel_id=1, source_target_pairs={{0,1},{1,0},{2,3},{3,2},{4,5},{5,4},{6,7},{7,6},{8,9},{9,8},{10,11... | collective-permute-start | bytes 1572872 | tf_op jit(solution)/shard_map/ppermute | solution.py:455
  51.1 30.7 %copy-start = (bf16[9,2,256,256]{3,2,1,0:T(8,128)(2,1)S(1)}, bf16[9,2,256,256]{3,2,1,0:T(8,128)(2,1)}, u32[]{:S(2)}) copy-start(bf16[9,2,256,256]{3,2,1,0:T(8,128)(2,1)} %constant.12.clone.table_ref.refs_12_) | copy-start | bytes 7077892
  53.2 26.7 %copy-start.3 = (bf16[16,128,128]{2,1,0:T(8,128)(2,1)}, bf16[16,128,128]{2,1,0:T(8,128)(2,1)S(1)}, u32[]{:S(2)}) copy-start(bf16[16,128,128]{2,1,0:T(8,128)(2,1)S(1)} %all-to-all-done.1) | copy-start | bytes 1572868
  53.2 47.6 %all-to-all-start = ((bf16[16,128,128]{2,1,0:T(8,128)(2,1)}), bf16[16,128,128]{2,1,0:T(8,128)(2,1)S(1)}, u32[]{:S(2)}, u32[]{:S(2)}) async-start(bf16[16,128,128]{2,1,0:T(8,128)(2,1)} %shard_map.126), calls=%async_computation | async-start | bytes 1048576 | tf_op jit(solution)/shard_map/all_to_all | solution.py:462
  62.5 13.6 %collective-permute-start.15 = (bf16[64,2048]{1,0:T(8,128)(2,1)}, bf16[64,2048]{1,0:T(8,128)(2,1)}, u32[]{:S(2)}, u32[]{:S(2)}) collective-permute-start(bf16[64,2048]{1,0:T(8,128)(2,1)} %shard_map.125), channel_id=1, source_target_pairs={{4,0},{5,1},{8,4},{9,5},{12,8},{13,9},{14,12},{15,13},{10,14},{11,... | collective-permute-start | bytes 786440 | tf_op jit(solution)/shard_map/ppermute | solution.py:498
  69.2 10.6 %collective-permute-start.13 = (bf16[64,2048]{1,0:T(8,128)(2,1)}, bf16[64,2048]{1,0:T(8,128)(2,1)}, u32[]{:S(2)}, u32[]{:S(2)}) collective-permute-start(bf16[64,2048]{1,0:T(8,128)(2,1)} %shard_map.124), channel_id=1, source_target_pairs={{0,4},{1,5},{4,8},{5,9},{8,12},{9,13},{12,14},{13,15},{14,10},{15,... | collective-permute-start | bytes 786440 | tf_op jit(solution)/shard_map/ppermute | solution.py:497
  69.2 25.7 %collective-permute-start.6 = (bf16[128,2048]{1,0:T(8,128)(2,1)}, bf16[128,2048]{1,0:T(8,128)(2,1)}, u32[]{:S(2)}, u32[]{:S(2)}) collective-permute-start(bf16[128,2048]{1,0:T(8,128)(2,1)} %collective-permute-done.5.refs_0_.refs_6_), channel_id=1, source_target_pairs={{0,1},{1,0},{2,3},{3,2},{4,5},{5,4},{6,7},{7,6},{8,9},{9,8},{10,11... | collective-permute-start | bytes 1572872 | tf_op jit(solution)/shard_map/ppermute | solution.py:455
  69.3 28.6 %collective-permute-start.12 = (bf16[128,2048]{1,0:T(8,128)(2,1)}, bf16[128,2048]{1,0:T(8,128)(2,1)}, u32[]{:S(2)}, u32[]{:S(2)}) collective-permute-start(bf16[128,2048]{1,0:T(8,128)(2,1)} %collective-permute-done.11.refs_2_.in_ref), channel_id=1, source_target_pairs={{0,1},{1,0},{2,3},{3,2},{4,5},{5,4},{6,7},{7,6},{8,9},{9,8},{10,11... | collective-permute-start | bytes 1572872 | tf_op jit(solution)/shard_map/ppermute | solution.py:455
  69.8 28.1 %collective-permute-start.10 = (bf16[128,2048]{1,0:T(8,128)(2,1)}, bf16[128,2048]{1,0:T(8,128)(2,1)}, u32[]{:S(2)}, u32[]{:S(2)}) collective-permute-start(bf16[128,2048]{1,0:T(8,128)(2,1)} %collective-permute-done.9.refs_0_.in_ref), channel_id=1, source_target_pairs={{0,1},{1,0},{2,3},{3,2},{4,5},{5,4},{6,7},{7,6},{8,9},{9,8},{10,11... | collective-permute-start | bytes 1572872 | tf_op jit(solution)/shard_map/ppermute | solution.py:455
  76.1 24.7 %collective-permute-start.16 = (bf16[64,2048]{1,0:T(8,128)(2,1)}, bf16[64,2048]{1,0:T(8,128)(2,1)}, u32[]{:S(2)}, u32[]{:S(2)}) collective-permute-start(bf16[64,2048]{1,0:T(8,128)(2,1)} %collective-permute-done.15.refs_6_.refs_2_), channel_id=1, source_target_pairs={{0,1},{1,0},{2,3},{3,2},{4,5},{5,4},{6,7},{7,6},{8,9},{9,8},{10,11... | collective-permute-start | bytes 786440 | tf_op jit(solution)/shard_map/ppermute | solution.py:455
  79.8 21.0 %collective-permute-start.14 = (bf16[64,2048]{1,0:T(8,128)(2,1)}, bf16[64,2048]{1,0:T(8,128)(2,1)}, u32[]{:S(2)}, u32[]{:S(2)}) collective-permute-start(bf16[64,2048]{1,0:T(8,128)(2,1)} %collective-permute-done.13.refs_4_.refs_0_), channel_id=1, source_target_pairs={{0,1},{1,0},{2,3},{3,2},{4,5},{5,4},{6,7},{7,6},{8,9},{9,8},{10,11... | collective-permute-start | bytes 786440 | tf_op jit(solution)/shard_map/ppermute | solution.py:455
  80.5 1.0 copy-start.10
  81.8 6.2 %copy-start.4 = (bf16[16,128,128]{2,1,0:T(8,128)(2,1)S(1)}, bf16[16,128,128]{2,1,0:T(8,128)(2,1)}, u32[]{:S(2)}) copy-start(bf16[16,128,128]{2,1,0:T(8,128)(2,1)} %copy-done.3) | copy-start | bytes 1572868
  95.0 5.8 %copy-start.7 = (bf16[512,128]{1,0:T(8,128)(2,1)S(1)}, bf16[512,128]{1,0:T(8,128)(2,1)}, u32[]{:S(2)}) copy-start(bf16[512,128]{1,0:T(8,128)(2,1)} %shard_map.121.refs_1_) | copy-start | bytes 393220
  100.8 1.0 copy-start.1
  101.8 0.9 copy-start.8
  110.6 36.0 %all-to-all-start.2 = ((bf16[16,2,128,128]{3,2,1,0:T(8,128)(2,1)}), bf16[16,2,128,128]{3,2,1,0:T(8,128)(2,1)}, u32[]{:S(2)}, u32[]{:S(2)}) async-start(bf16[16,2,128,128]{3,2,1,0:T(8,128)(2,1)} %get-tuple-element.13), calls=%async_computation.2 | async-start | bytes 2097152 | tf_op jit(solution)/shard_map/all_to_all | solution.py:462
  115.8 5.8 %copy-start.2 = (bf16[2048,128]{1,0:T(8,128)(2,1)S(1)}, bf16[2048,128]{1,0:T(8,128)(2,1)}, u32[]{:S(2)}) copy-start(bf16[2048,128]{1,0:T(8,128)(2,1)} %get-tuple-element.12.refs_10_.refs_11_.refs_5_) | copy-start | bytes 1572868
  120.0 14.9 %collective-permute-start.17 = (bf16[128,2048]{1,0:T(8,128)(2,1)S(1)}, bf16[128,2048]{1,0:T(8,128)(2,1)S(1)}, u32[]{:S(2)}, u32[]{:S(2)}) collective-permute-start(bf16[128,2048]{1,0:T(8,128)(2,1)S(1)} %shard_map.132), channel_id=1, source_target_pairs={{0,16},{16,0},{1,17},{17,1},{2,18},{18,2},{3,19},{19,3},{4,20},{20... | collective-permute-start | bytes 1572872 | tf_op jit(solution)/shard_map/ppermute | solution.py:572
  128.5 18.0 %copy-start.5 = (bf16[1,128,2048]{2,1,0:T(8,128)(2,1)S(1)}, bf16[1,128,2048]{2,1,0:T(8,128)(2,1)}, u32[]{:S(2)}) copy-start(bf16[1,128,2048]{2,1,0:T(8,128)(2,1)} %param.9) | copy-start | bytes 1572868
  128.6 18.0 %copy-start.6 = (bf16[1,128,2048]{2,1,0:T(8,128)(2,1)S(1)}, bf16[1,128,2048]{2,1,0:T(8,128)(2,1)}, u32[]{:S(2)}) copy-start(bf16[1,128,2048]{2,1,0:T(8,128)(2,1)} %param.10) | copy-start | bytes 1572868
  128.6 16.9 %collective-permute-start.18 = (bf16[128,2048]{1,0:T(8,128)(2,1)S(1)}, bf16[128,2048]{1,0:T(8,128)(2,1)S(1)}, u32[]{:S(2)}, u32[]{:S(2)}) collective-permute-start(bf16[128,2048]{1,0:T(8,128)(2,1)S(1)} %shard_map.135), channel_id=1, source_target_pairs={{0,16},{16,0},{1,17},{17,1},{2,18},{18,2},{3,19},{19,3},{4,20},{20... | collective-permute-start | bytes 1572872 | tf_op jit(solution)/shard_map/ppermute | solution.py:572
  (2 other events, 1.7 us)
